TPU v7x, 256 devices: a whole 4x4x8 slice. The times are simulated.
256 devices in a mesh: depth: 8 (over z), col: 4 (over y), row: 8 (over x, core).
Axes of the slice: x: 4, y: 4, z: 8, core: 2. Of those that a mesh axis runs over, the one named last changes fastest.
Arguments:
- a_mat: bfloat16 [16384, 16384], P('row', 'col')
- b_mat: bfloat16 [16384, 16384], P('row', 'col')
Outputs:
- output: bfloat16 [16384, 16384], P(('row', 'depth'), 'col')
All inputs are finite; a program needn't handle non-finite values.
Results may differ from a plain program's by a relative error of at most 0.001.
Values are sent between devices in bfloat16 or wider.
A program may use at most 768 MiB of HBM per device.

v0:
```python
import jax
import jax.numpy as jnp
from jax import lax
from jax.sharding import PartitionSpec as P

AXES_ALL = ("depth", "col", "row")


def skew_pairs(depth_n, col_n, row_n):
    col_ratio = row_n // col_n
    layer_steps = row_n // depth_n
    pairs_a0 = []
    pairs_a1 = []
    pairs_b = []
    for layer_idx in range(depth_n):
        for col_idx in range(col_n):
            for row_idx in range(row_n):
                target_dev = (layer_idx * col_n + col_idx) * row_n + row_idx
                start_blk = (row_idx + col_ratio * col_idx + layer_idx * layer_steps) % row_n
                coarse_blk = start_blk // col_ratio
                pairs_a0.append(((layer_idx * col_n + coarse_blk) * row_n + row_idx, target_dev))
                pairs_a1.append(((layer_idx * col_n + (coarse_blk + 1) % col_n) * row_n + row_idx, target_dev))
                pairs_b.append(((layer_idx * col_n + col_idx) * row_n + start_blk, target_dev))
    return pairs_a0, pairs_a1, pairs_b


def solution(mesh):
    depth_n = mesh.shape["depth"]
    col_n = mesh.shape["col"]
    row_n = mesh.shape["row"]
    col_ratio = row_n // col_n
    layer_steps = row_n // depth_n
    pairs_a0, pairs_a1, pairs_b = skew_pairs(depth_n, col_n, row_n)
    pairs_col = [((col_idx + 1) % col_n, col_idx) for col_idx in range(col_n)]
    pairs_row = [((row_idx + 1) % row_n, row_idx) for row_idx in range(row_n)]

    def local_mm(a_blk, b_blk):
        layer_idx = lax.axis_index("depth")
        row_idx = lax.axis_index("row")
        fine_side = a_blk.shape[0]
        a_first = lax.ppermute(a_blk, AXES_ALL, pairs_a0)
        if col_ratio > 1:
            a_second = lax.ppermute(a_blk, AXES_ALL, pairs_a1)
            a_joined = jnp.concatenate([a_first, a_second], axis=1)
            offset = ((row_idx + layer_idx * layer_steps) % col_ratio) * fine_side
            a_window = lax.dynamic_slice_in_dim(a_joined, offset, a_blk.shape[1], axis=1)
        else:
            a_window = a_first
        a_parts = [a_window[:, blk_idx * fine_side:(blk_idx + 1) * fine_side] for blk_idx in range(min(col_ratio, layer_steps))]
        b_cur = lax.ppermute(b_blk, AXES_ALL, pairs_b)
        part_sum = None
        for step_idx in range(layer_steps):
            a_cur = a_parts[step_idx]
            block_prod = jnp.dot(a_cur, b_cur, preferred_element_type=jnp.float32)
            part_sum = block_prod if part_sum is None else part_sum + block_prod
            if step_idx + col_ratio < layer_steps:
                a_parts.append(lax.ppermute(a_cur, "col", pairs_col))
            if step_idx + 1 < layer_steps:
                b_cur = lax.ppermute(b_cur, "row", pairs_row)
        c_rows = lax.psum_scatter(part_sum, "depth", scatter_dimension=0, tiled=True)
        return c_rows.astype(jnp.bfloat16)

    spec_in = P("row", "col")
    spec_out = P(("row", "depth"), "col")
    return jax.shard_map(local_mm, mesh=mesh, in_specs=(spec_in, spec_in), out_specs=spec_out, check_vma=False)
```

profile of v0, /device:TPU:1, one launch (start us, length us, event | category | flops | bytes accessed | tf_op | source)
XLA Modules:
  0.0 1247.7 jit_solution(12120906799677201705)
XLA Ops:
  6.5 0.0 reduce-scatter.2.cloned.1.call-start
  6.5 126.6 %collective-permute-start.2 = (bf16[2048,4096]{1,0:T(8,128)(2,1)}, bf16[2048,4096]{1,0:T(8,128)(2,1)}, u32[]{:S(2)}, u32[]{:S(2)}) collective-permute-start(bf16[2048,4096]{1,0:T(8,128)(2,1)} %param.3), channel_id=1, source_target_pairs={{0,0},{1,1},{2,2},{3,3},{4,4},{5,5},{6,6},{7,7},{10,8},{11,9},{12,... | collective-permute-start | bytes 50331656 | tf_op jit(solution)/shard_map/ppermute | solution.py:50
  133.1 1.9 collective-permute-start.1
  135.0 126.6 %collective-permute-start = (bf16[2048,4096]{1,0:T(8,128)(2,1)}, bf16[2048,4096]{1,0:T(8,128)(2,1)}, u32[]{:S(2)}, u32[]{:S(2)}) collective-permute-start(bf16[2048,4096]{1,0:T(8,128)(2,1)} %param.2), channel_id=1, source_target_pairs={{0,0},{1,1},{10,2},{11,3},{20,4},{21,5},{30,6},{31,7},{8,8},{9,9},... | collective-permute-start | bytes 50331656 | tf_op jit(solution)/shard_map/ppermute | solution.py:41
  261.7 0.0 collective-permute-done.2
  261.7 232.0 %collective-permute-done.1 = bf16[2048,4096]{1,0:T(8,128)(2,1)} collective-permute-done((bf16[2048,4096]{1,0:T(8,128)(2,1)}, bf16[2048,4096]{1,0:T(8,128)(2,1)}, u32[]{:S(2)}, u32[]{:S(2)}) %collective-permute-start.1) | collective-permute-done | bytes 16777248 | tf_op jit(solution)/shard_map/ppermute | solution.py:43
  493.7 0.0 collective-permute-done
  493.7 45.0 %fusion.1 = f32[2048,4096]{1,0:T(8,128)} fusion(bf16[2048,4096]{1,0:T(8,128)(2,1)} %collective-permute-done.2, s32[]{:T(128)S(6)} %select_n.11, bf16[2048,4096]{1,0:T(8,128)(2,1)} %collective-permute-done, bf16[2048,4096]{1,0:T(8,128)(2,1)} %collective-permute-done.1), kind=kOutput, calls=%fused_computation.3 | convolution fusion | flops 34376515584 | bytes 83886080 | tf_op jit(solution)/shard_map/dot_general | solution.py:54
  538.7 0.0 reduce-scatter.2.cloned.1.call-update
  538.7 698.3 %reduce-scatter.2.cloned.1.call-done = f32[256,4096]{1,0:T(8,128)} async-done(((f32[2048,4096]{1,0:T(8,128)}), f32[256,4096]{1,0:T(8,128)}) %reduce-scatter.2.cloned.1.call-update) | async-done | bytes 4194320 | tf_op jit(solution)/shard_map/reduce_scatter | solution.py:60
  1237.1 3.8 convert_element_type.3
Async XLA Ops:
  6.5 1230.5 %reduce-scatter.2.cloned.1.call-start = ((), (), s32[]{:S(2)}) async-start(), calls=%async_computation.1 | async-start | bytes 37748736 | tf_op jit(solution)/shard_map/reduce_scatter | solution.py:60
  6.5 255.1 %collective-permute-start.2 = (bf16[2048,4096]{1,0:T(8,128)(2,1)}, bf16[2048,4096]{1,0:T(8,128)(2,1)}, u32[]{:S(2)}, u32[]{:S(2)}) collective-permute-start(bf16[2048,4096]{1,0:T(8,128)(2,1)} %param.3), channel_id=1, source_target_pairs={{0,0},{1,1},{2,2},{3,3},{4,4},{5,5},{6,6},{7,7},{10,8},{11,9},{12,... | collective-permute-start | bytes 50331656 | tf_op jit(solution)/shard_map/ppermute | solution.py:50
  133.1 360.6 %collective-permute-start.1 = (bf16[2048,4096]{1,0:T(8,128)(2,1)}, bf16[2048,4096]{1,0:T(8,128)(2,1)}, u32[]{:S(2)}, u32[]{:S(2)}) collective-permute-start(bf16[2048,4096]{1,0:T(8,128)(2,1)} %param.2), channel_id=1, source_target_pairs={{8,0},{9,1},{18,2},{19,3},{28,4},{29,5},{6,6},{7,7},{16,8},{17,9},... | collective-permute-start | bytes 50331656 | tf_op jit(solution)/shard_map/ppermute | solution.py:43
  135.0 358.7 %collective-permute-start = (bf16[2048,4096]{1,0:T(8,128)(2,1)}, bf16[2048,4096]{1,0:T(8,128)(2,1)}, u32[]{:S(2)}, u32[]{:S(2)}) collective-permute-start(bf16[2048,4096]{1,0:T(8,128)(2,1)} %param.2), channel_id=1, source_target_pairs={{0,0},{1,1},{10,2},{11,3},{20,4},{21,5},{30,6},{31,7},{8,8},{9,9},... | collective-permute-start | bytes 50331656 | tf_op jit(solution)/shard_map/ppermute | solution.py:41
Sparse Core Ops, SparseCore 0:
  538.9 698.1 reduce-scatter.1
where the time goes:
time: 1270 us; the launch traced here: 1250 us
  waiting for transfers between devices  930 us (73%)
  starting transfers between devices  255 us (20%)
  matrix products  45 us (4%)
  between operations  13.4 us (1%)
    reduce_scatter x1, waiting for transfers between devices, local_mm(): lax.psum_scatter(part_sum, 'depth', scatter_dimension=0, tiled=True)  698 us
    ppermute x1, waiting for transfers between devices, local_mm(): a_second = lax.ppermute(a_blk, AXES_ALL, pairs_a1)  232 us
    ppermute x1, starting transfers between devices, local_mm(): a_first = lax.ppermute(a_blk, AXES_ALL, pairs_a0)  127 us
    ppermute x1, starting transfers between devices, local_mm(): b_cur = lax.ppermute(b_blk, AXES_ALL, pairs_b)  127 us
    dot_general x1, matrix products, local_mm(): block_prod = jnp.dot(a_cur, b_cur, preferred_element_type=jnp.float32)  45 us
  transfers between devices with their start and end apart: 4, of which 2 were waited for; matrix products, arithmetic and copies ran while one was open for 0% of the time, Pallas kernels for 0%

commit v1 on v0

v1 whole, which is shorter than its diff:
```python
import functools

import jax
import jax.numpy as jnp
from jax import lax
from jax.experimental import pallas as pl
from jax.experimental.pallas import tpu as pltpu
from jax.sharding import PartitionSpec as P

MESH = pl.DeviceIdType.MESH
NX = 4
NS = 2
ORDER = [(2, 0), (2, 1), (1, 0), (3, 0), (1, 1), (3, 1), (0, 0), (0, 1)]


def chunk_order(nz):
    return sorted(range(nz), key=lambda r: -min(r, nz - r))


def kernel(nz, ny, a_ref, b_ref, o_ref, abuf, bbuf, ro, rn, pbuf, obuf,
           a_sem, s1_send, b_recv, ag_send, fw_send, op_send, op_recv, nb_send, nb_recv, out_send, out_recv):
    z = lax.axis_index("depth")
    y = lax.axis_index("col")
    i = lax.axis_index("row")
    x, c = i // 2, i % 2
    rows, depth_k = abuf.shape
    half_k = depth_k // 2
    quarter = half_k // NX
    width = depth_k // nz
    sub = width // NS
    chunk = rows // nz
    mblk = rows // 4
    order_z = chunk_order(nz)

    def dev(zz, yy, xx, cc):
        return ((zz + nz) % nz, (yy + ny) % ny, 2 * ((xx + NX) % NX) + cc)

    def remote(src, dst, send_sem, recv_sem, device):
        return pltpu.make_async_remote_copy(src_ref=src, dst_ref=dst, send_sem=send_sem, recv_sem=recv_sem,
                                            device_id=device, device_id_type=MESH)

    sibling = dev(z, y, x, 1 - c)

    a_copies = [pltpu.make_async_copy(a_ref.at[pl.ds(m * mblk, mblk)], abuf.at[pl.ds(m * mblk, mblk)], a_sem.at[m])
                for m in range(4)]
    for cp in a_copies:
        cp.start()

    barrier = pltpu.get_barrier_semaphore()
    partners = [sibling]
    partners += [dev(z, y + dy, x + dx, c) for dy in range(ny) for dx in range(NX) if dx or dy]
    partners += [dev(z + r, y, x, c) for r in range(1, nz)]
    for p in partners:
        pl.semaphore_signal(barrier, inc=1, device_id=p, device_id_type=MESH)
    pl.semaphore_wait(barrier, len(partners))

    t_me = (y - x + NX) % NX

    def piece(t, s, lane, q):
        return bbuf.at[t, s, pl.ds(lane * half_k + q * quarter, quarter)]

    def stage1(s, q, local, act):
        src = b_ref.at[pl.ds(q * quarter, quarter), pl.ds(pl.multiple_of(z * width + s * sub, sub), sub)]
        dst, sem = piece(t_me, s, c, q), b_recv.at[t_me, s, c * NX + q]
        if local:
            act(pltpu.make_async_copy(src, dst, sem))
        else:
            act(remote(src, dst, s1_send.at[s, q], sem, dev(z, x, q, c)))

    def own_piece(q):
        return (x == y) & (x == q)

    def stage1_start():
        for s in range(NS):
            for q in range(NX):
                @pl.when(jnp.logical_not(own_piece(q)))
                def _():
                    stage1(s, q, False, lambda cp: cp.start())

                @pl.when(own_piece(q))
                def _():
                    stage1(s, q, True, lambda cp: cp.start())

    def arrived(t, s, lane, q):
        ref = piece(t, s, lane, q)
        remote(ref, ref, fw_send.at[t, s, 0], b_recv.at[t, s, lane * NX + q], sibling).wait_recv()

    def gather_copies(t, s):
        ref = piece(t, s, c, x)
        sem = b_recv.at[t, s, c * NX + x]
        out = [remote(ref, ref, ag_send.at[t, s, d], sem, dev(z, y, x + d, c)) for d in (1, 3, 2)]
        out.append(remote(ref, ref, ag_send.at[t, s, 0], sem, sibling))
        return out

    def gather(t, s):
        arrived(t, s, c, x)
        for cp in gather_copies(t, s):
            cp.start()

    def forward_copies(t, s):
        for d in (1, 3, 2):
            q = (x + d) % NX
            ref = piece(t, s, c, q)
            yield q, remote(ref, ref, fw_send.at[t, s, d - 1], b_recv.at[t, s, c * NX + q], sibling)

    def forward(t, s):
        for q, cp in forward_copies(t, s):
            arrived(t, s, c, q)
            cp.start()

    def matmul(t, s, slot):
        for q in range(NX):
            arrived(t, s, 1 - c, q)

        def body(m, carry):
            r = pl.ds(pl.multiple_of(m * mblk, mblk), mblk)
            pbuf[slot, s, r, :] = jnp.dot(abuf[r, :], bbuf[t, s], preferred_element_type=jnp.float32)
            return carry

        lax.fori_loop(0, 4, body, 0)

    half = rows // 2

    def opposite_copy(s, d):
        return remote(pbuf.at[0, s, pl.ds(d * half, half)], ro.at[d, s], op_send.at[d, s], op_recv.at[d, s],
                      dev(z, y + 1 - 2 * d, x, c))

    def merge(d, s):
        opposite_copy(s, d).wait_recv()

        def body(m, carry):
            r = pl.ds(pl.multiple_of(m * (half // 4), half // 4), half // 4)
            rp = pl.ds(pl.multiple_of(d * half + m * (half // 4), half // 4), half // 4)
            pbuf[1 + d, s, rp, :] = pbuf[1 + d, s, rp, :] + ro[d, s, r, :]
            return carry

        lax.fori_loop(0, 4, body, 0)

    def chunk_rows(r):
        zz = (z + r) % nz
        return pl.ds(pl.multiple_of(zz * chunk, chunk), chunk)

    def neighbour_copy(d, s, r):
        cr = chunk_rows(r)
        return remote(pbuf.at[1 + d, s, cr], rn.at[d, s, cr], nb_send.at[d, s, r], nb_recv.at[d, s, r],
                      dev(z, y + 1 - 2 * d, x, c))

    def send_neighbours(s):
        for r in order_z:
            for d in (0, 1):
                neighbour_copy(d, s, r).start()

    def out_copy(s, r):
        cols = pl.ds(pl.multiple_of(z * width + s * sub, sub), sub)
        if r == 0:
            return pltpu.make_async_copy(obuf.at[s, chunk_rows(0)], o_ref.at[:, cols], out_recv.at[s, 0])
        return remote(obuf.at[s, chunk_rows(r)], o_ref.at[:, cols], out_send.at[s, r], out_recv.at[s, r],
                      dev(z + r, y, x, c))

    def out_arrived(s, r):
        if r == 0:
            out_copy(s, 0).wait()
            return
        src_z = (z - r + nz) % nz
        cols = pl.ds(pl.multiple_of(src_z * width + s * sub, sub), sub)
        remote(obuf.at[s, chunk_rows(r)], o_ref.at[:, cols], out_send.at[s, r], out_recv.at[s, r],
               dev(z + r, y, x, c)).wait_recv()

    def finish(s):
        for r in order_z:
            for d in (0, 1):
                neighbour_copy(d, s, r).wait_recv()
            cr = chunk_rows(r)
            total = pbuf[0, s, cr, :] + rn[0, s, cr, :] + rn[1, s, cr, :]
            obuf[s, cr, :] = total.astype(jnp.bfloat16)
            out_copy(s, r).start()

    slot_of = {2: 0, 1: 1, 3: 2, 0: 0}

    @pl.when(t_me == 2)
    def _():
        stage1_start()

    gather(*ORDER[0])

    @pl.when(t_me != 2)
    def _():
        stage1_start()

    gather(*ORDER[1])
    for cp in a_copies:
        cp.wait()
    for n, (t, s) in enumerate(ORDER):
        forward(t, s)
        if t == 0:
            for d in (0, 1):
                opposite_copy(s, d).wait_send()
        matmul(t, s, slot_of[t])
        if t == 2:
            for d in (0, 1):
                opposite_copy(s, d).start()
        if t == 3:
            merge(0, s)
            merge(1, s)
            send_neighbours(s)
        if n + 2 < len(ORDER):
            gather(*ORDER[n + 2])
    for s in range(NS):
        finish(s)

    for s in range(NS):
        for q in range(NX):
            @pl.when(jnp.logical_not(own_piece(q)))
            def _():
                stage1(s, q, False, lambda cp: cp.wait_send())
    for t, s in ORDER:
        for cp in gather_copies(t, s):
            cp.wait_send()
        for _, cp in forward_copies(t, s):
            cp.wait_send()
    for s in range(NS):
        for r in order_z:
            for d in (0, 1):
                neighbour_copy(d, s, r).wait_send()
            if r:
                out_copy(s, r).wait_send()
            out_arrived(s, r)


def local_product(nz, ny, a_blk, b_blk):
    rows, depth_k = a_blk.shape
    half_k = b_blk.shape[0]
    sub = depth_k // nz // NS
    f32, bf16 = jnp.float32, jnp.bfloat16
    dma = pltpu.SemaphoreType.DMA
    return pl.pallas_call(
        functools.partial(kernel, nz, ny),
        name="stationary_a",
        out_shape=jax.ShapeDtypeStruct((rows // nz, depth_k), bf16),
        in_specs=[pl.BlockSpec(memory_space=pl.ANY)] * 2,
        out_specs=pl.BlockSpec(memory_space=pl.ANY),
        scratch_shapes=[
            pltpu.VMEM((rows, depth_k), bf16),
            pltpu.VMEM((NX, NS, 2 * half_k, sub), bf16),
            pltpu.VMEM((2, NS, rows // 2, sub), f32),
            pltpu.VMEM((2, NS, rows, sub), f32),
            pltpu.VMEM((3, NS, rows, sub), f32),
            pltpu.VMEM((NS, rows, sub), bf16),
            dma((4,)),
            dma((NS, NX)),
            dma((NX, NS, 2 * NX)),
            dma((NX, NS, 4)),
            dma((NX, NS, 3)),
            dma((2, NS)),
            dma((2, NS)),
            dma((2, NS, nz)),
            dma((2, NS, nz)),
            dma((NS, nz)),
            dma((NS, nz)),
        ],
        compiler_params=pltpu.CompilerParams(collective_id=0, has_side_effects=True, vmem_limit_bytes=67043328),
    )(a_blk, b_blk)


def solution(mesh):
    nz, ny = mesh.shape["depth"], mesh.shape["col"]
    return jax.shard_map(
        functools.partial(local_product, nz, ny),
        mesh=mesh,
        in_specs=(P("row", "col"), P("row", "col")),
        out_specs=P(("row", "depth"), "col"),
        check_vma=False,
    )
```

time: 1270 us -> 201 us (0.16); the launches traced: 1250 us -> 201 us
  waiting for transfers between devices: 930 us -> 0 us
  starting transfers between devices: 255 us -> 0 us
  Pallas kernels: 0 us -> 198 us
  matrix products: 45 us -> 0 us
  between operations: 13.4 us -> 0.01 us
    reduce_scatter x1 -> x0, waiting for transfers between devices: 698 us -> none  [local_mm(): lax.psum_scatter(part_sum, 'depth', scatter_dimension=0, tiled=True)]
    ppermute x3 -> x0, starting transfers between devices: 255 us -> none  [the longest x1 127 us: local_mm(): a_first = lax.ppermute(a_blk, AXES_ALL, pairs_a0)]
    ppermute x3 -> x0, waiting for transfers between devices: 232 us -> none  [the longest x1 232 us: local_mm(): a_second = lax.ppermute(a_blk, AXES_ALL, pairs_a1)]
    pallas_call x0 -> x1, Pallas kernels: none -> 198 us  [local_product(): pl.pallas_call(functools.partial(kernel, nz, ny), name='stationary_a', ou...]
    dot_general x1 -> x0, matrix products: 45 us -> none  [local_mm(): block_prod = jnp.dot(a_cur, b_cur, preferred_element_type=jnp.float32)]
  transfers between devices with their start and end apart: 4 -> 0, of which waited for: 2 -> 0; matrix products, arithmetic and copies ran while one was open for 0% -> 0% of each run, Pallas kernels for 0% -> 0%
where the time goes in v1:
time: 201 us
  Pallas kernels  198 us (99%)
  local copies, waits for them, and re-layouts  3.13 us (2%)
    pallas_call x1, Pallas kernels, local_product(): pl.pallas_call(functools.partial(kernel, nz, ny), name='stationary_a', ou...  198 us

profile of v1, /device:TPU:1, one launch (start us, length us, event | category | flops | bytes accessed | tf_op | source)
XLA Modules:
  0.0 200.8 jit_solution(3298651615184967535)
XLA Ops:
  0.0 197.6 %stationary_a.1 = bf16[256,4096]{1,0:T(8,128)(2,1)} custom-call(bf16[2048,4096]{1,0:T(8,128)(2,1)} %a_ref.1, bf16[2048,4096]{1,0:T(8,128)(2,1)} %b_ref.1), custom_call_target="tpu_custom_call" | custom-call | tf_op jit(solution)/shard_map/stationary_a/pallas_call | solution.py:236
  197.6 3.1 %copy.4 = bf16[256,4096]{1,0:T(8,128)(2,1)} copy(bf16[256,4096]{1,0:T(8,128)(2,1)} %stationary_a.1) | data formatting | bytes 4194304

commit v2 on v1

v2 whole, which is shorter than its diff:
```python
import functools

import jax
import jax.numpy as jnp
from jax import lax
from jax.experimental import pallas as pl
from jax.experimental.pallas import tpu as pltpu
from jax.sharding import PartitionSpec as P

MESH = pl.DeviceIdType.MESH
NX = 4
PIECES = [(2, 0, 4), (2, 4, 4), (2, 8, 8), (1, 0, 8), (3, 0, 8), (1, 8, 8), (3, 8, 8), (0, 0, 16)]
OPPOSITE = [0, 1, 2]
HALVES = [(0, 8), (8, 8)]
SLOT = {2: 0, 1: 1, 3: 2, 0: 0}
SCRIPT = """S2:0 S2:1 S2:2 G0 S1:3 S3:4 G1 L0 R0 L1 R1 O0 G2 C0a L2 R2 C0b O1 C1a S1:5 S3:6 G3 C1b G4 O2 C2a L3 R3 C2b L4 R4 O3 S0:7
C3a G5 C3b O4 C4a G6 C4b M0 L5 R5 L6 R6 O5 C5a G7 C5b O6 C6a L7 R7 C6b M1 O7 C7a C7b F0 F1"""


def chunk_order(nz):
    return sorted(range(nz), key=lambda r: -min(r, nz - r))


def kernel(nz, ny, a_ref, b_ref, o_ref, abuf, bbuf, ro, rn, pbuf, obuf,
           a_sem, s1_send, b_recv, ag_send, fw_send, op_send, op_recv, nb_send, nb_recv, out_send, out_recv):
    z = lax.axis_index("depth")
    y = lax.axis_index("col")
    i = lax.axis_index("row")
    x, c = i // 2, i % 2
    rows, depth_k = abuf.shape
    half_k = depth_k // 2
    quarter = half_k // NX
    width = depth_k // nz
    unit = width // 16
    chunk = rows // nz
    mblk = rows // 4
    half = rows // 2
    order_z = chunk_order(nz)

    def dev(zz, yy, xx, cc):
        return ((zz + nz) % nz, (yy + ny) % ny, 2 * ((xx + NX) % NX) + cc)

    def remote(src, dst, send_sem, recv_sem, device):
        return pltpu.make_async_remote_copy(src_ref=src, dst_ref=dst, send_sem=send_sem, recv_sem=recv_sem,
                                            device_id=device, device_id_type=MESH)

    sibling = dev(z, y, x, 1 - c)
    left, right = dev(z, y, x - 1, c), dev(z, y, x + 1, c)

    a_copies = [pltpu.make_async_copy(a_ref.at[pl.ds(m * mblk, mblk)], abuf.at[pl.ds(m * mblk, mblk)], a_sem.at[m])
                for m in range(4)]
    for cp in a_copies:
        cp.start()

    barrier = pltpu.get_barrier_semaphore()
    partners = [sibling]
    partners += [dev(z, y + dy, x + dx, c) for dy in range(ny) for dx in range(NX) if dx or dy]
    partners += [dev(z + r, y, x, c) for r in range(1, nz)]
    for p in partners:
        pl.semaphore_signal(barrier, inc=1, device_id=p, device_id_type=MESH)
    pl.semaphore_wait(barrier, len(partners))

    t_me = (y - x + NX) % NX

    def columns(n):
        return pl.ds(PIECES[n][1] * unit, PIECES[n][2] * unit)

    def stage1(n, q, local, act):
        t, first, wide = PIECES[n]
        cols = pl.ds(pl.multiple_of(z * width + first * unit, 4 * unit), wide * unit)
        src = b_ref.at[pl.ds(q * quarter, quarter), cols]
        dst = bbuf.at[t, pl.ds(pl.multiple_of(c * half_k + q * quarter, quarter), quarter), columns(n)]
        sem = b_recv.at[n, c * 5]
        if local:
            act(pltpu.make_async_copy(src, dst, sem))
        else:
            act(remote(src, dst, s1_send.at[n, q], sem, dev(z, x, q, c)))

    def stage1_all(n, act, with_local):
        for q in range(NX):
            if PIECES[n][0]:
                stage1(n, q, False, act)
            else:
                @pl.when(x != q)
                def _():
                    stage1(n, q, False, act)

                if with_local:
                    @pl.when(x == q)
                    def _():
                        stage1(n, q, True, act)

    def part(n, lane, k):
        q = (x + (0, 3, 1, 2, 2)[k]) % NX
        start, size = lane * half_k + q * quarter, quarter
        if k >= 3:
            size = quarter // 2
            start = start + (k - 3) * size
        return bbuf.at[PIECES[n][0], pl.ds(pl.multiple_of(start, size), size), columns(n)]

    def arrived(n, lane, k):
        ref = part(n, lane, k)
        remote(ref, ref, fw_send.at[n, 0], b_recv.at[n, lane * 5 + k], sibling).wait_recv()

    def to_sibling(n, k):
        ref = part(n, c, k)
        return remote(ref, ref, fw_send.at[n, k], b_recv.at[n, c * 5 + k], sibling)

    def to_side(n, which):
        if which < 2:
            ref = part(n, c, 0)
        else:
            q = (x + (3, 1)[which - 2]) % NX
            size = quarter // 2
            start = c * half_k + q * quarter + (which - 2) * size
            ref = bbuf.at[PIECES[n][0], pl.ds(pl.multiple_of(start, size), size), columns(n)]
        return remote(ref, ref, ag_send.at[n, which], b_recv.at[n, c * 5 + 1 + which], (right, left)[which % 2])

    def pass_own(n):
        arrived(n, c, 0)
        to_side(n, 0).start()
        to_side(n, 1).start()
        to_sibling(n, 0).start()

    def pass_side(n, k):
        arrived(n, c, k)
        to_side(n, k + 1).start()
        to_sibling(n, k).start()

    def pass_far(n):
        for k in (3, 4):
            arrived(n, c, k)
            to_sibling(n, k).start()

    def opposite_copy(n, d):
        return remote(pbuf.at[0, pl.ds(d * half, half), columns(n)], ro.at[d, :, columns(n)],
                      op_send.at[n, d], op_recv.at[n, d], dev(z, y + 1 - 2 * d, x, c))

    def half_matmul(n, h):
        t = PIECES[n][0]
        if h == 0:
            for k in range(5):
                arrived(n, 1 - c, k)
            if n == 0:
                for cp in a_copies:
                    cp.wait()
            if t == 0:
                for m in OPPOSITE:
                    for d in (0, 1):
                        opposite_copy(m, d).wait_send()

        def body(m, carry):
            r = pl.ds(pl.multiple_of(m * mblk, mblk), mblk)
            pbuf[SLOT[t], r, columns(n)] = jnp.dot(abuf[r, :], bbuf[t, :, columns(n)],
                                                   preferred_element_type=jnp.float32)
            return carry

        lax.fori_loop(2 * h, 2 * h + 2, body, 0)
        if t == 2:
            opposite_copy(n, h).start()

    def chunk_rows(r):
        zz = (z + r) % nz
        return pl.ds(pl.multiple_of(zz * chunk, chunk), chunk)

    def half_columns(s):
        return pl.ds(HALVES[s][0] * unit, HALVES[s][1] * unit)

    def neighbour_copy(d, s, r):
        cr, cols = chunk_rows(r), half_columns(s)
        return remote(pbuf.at[1 + d, cr, cols], rn.at[d, cr, cols], nb_send.at[d, s, r], nb_recv.at[d, s, r],
                      dev(z, y + 1 - 2 * d, x, c))

    def merge(s):
        first, wide = HALVES[s]
        cols = half_columns(s)
        for n in OPPOSITE:
            if first <= PIECES[n][1] < first + wide:
                for d in (0, 1):
                    opposite_copy(n, d).wait_recv()
        for d in (0, 1):
            def body(m, carry):
                r = pl.ds(pl.multiple_of(m * (half // 4), half // 4), half // 4)
                rp = pl.ds(pl.multiple_of(d * half + m * (half // 4), half // 4), half // 4)
                pbuf[1 + d, rp, cols] = pbuf[1 + d, rp, cols] + ro[d, r, cols]
                return carry

            lax.fori_loop(0, 4, body, 0)
        for r in order_z:
            for d in (0, 1):
                neighbour_copy(d, s, r).start()

    def out_columns(zz, s):
        return pl.ds(pl.multiple_of(zz * width + HALVES[s][0] * unit, 8 * unit), HALVES[s][1] * unit)

    def out_copy(s, r):
        src = obuf.at[chunk_rows(r), half_columns(s)]
        if r == 0:
            return pltpu.make_async_copy(src, o_ref.at[:, out_columns(z, s)], out_recv.at[s, 0])
        return remote(src, o_ref.at[:, out_columns(z, s)], out_send.at[s, r], out_recv.at[s, r], dev(z + r, y, x, c))

    def out_arrived(s, r):
        if r == 0:
            out_copy(s, 0).wait()
        else:
            remote(obuf.at[chunk_rows(r), half_columns(s)], o_ref.at[:, out_columns((z - r + nz) % nz, s)],
                   out_send.at[s, r], out_recv.at[s, r], dev(z + r, y, x, c)).wait_recv()

    def finish(s):
        cols = half_columns(s)
        for r in order_z:
            for d in (0, 1):
                neighbour_copy(d, s, r).wait_recv()
            cr = chunk_rows(r)
            total = pbuf[0, cr, cols] + rn[0, cr, cols] + rn[1, cr, cols]
            obuf[cr, cols] = total.astype(jnp.bfloat16)
            out_copy(s, r).start()

    for item in SCRIPT.split():
        op, rest = item[0], item[1:]
        if op == "S":
            t, n = (int(v) for v in rest.split(":"))

            @pl.when(t_me == t)
            def _():
                stage1_all(n, lambda cp: cp.start(), True)
        elif op == "G":
            pass_own(int(rest))
        elif op == "L":
            pass_side(int(rest), 1)
        elif op == "R":
            pass_side(int(rest), 2)
        elif op == "O":
            pass_far(int(rest))
        elif op == "C":
            half_matmul(int(rest[0]), "ab".index(rest[1]))
        elif op == "M":
            merge(int(rest))
        elif op == "F":
            finish(int(rest))

    for n in range(len(PIECES)):
        @pl.when(t_me == PIECES[n][0])
        def _():
            stage1_all(n, lambda cp: cp.wait_send(), False)

        for which in range(4):
            to_side(n, which).wait_send()
        for k in range(5):
            to_sibling(n, k).wait_send()
    for s in range(len(HALVES)):
        for r in order_z:
            for d in (0, 1):
                neighbour_copy(d, s, r).wait_send()
            if r:
                out_copy(s, r).wait_send()
            out_arrived(s, r)


def local_product(nz, ny, a_blk, b_blk):
    rows, depth_k = a_blk.shape
    half_k = b_blk.shape[0]
    width = depth_k // nz
    f32, bf16 = jnp.float32, jnp.bfloat16
    dma = pltpu.SemaphoreType.DMA
    n = len(PIECES)
    return pl.pallas_call(
        functools.partial(kernel, nz, ny),
        name="stationary_a",
        out_shape=jax.ShapeDtypeStruct((rows // nz, depth_k), bf16),
        in_specs=[pl.BlockSpec(memory_space=pl.ANY)] * 2,
        out_specs=pl.BlockSpec(memory_space=pl.ANY),
        scratch_shapes=[
            pltpu.VMEM((rows, depth_k), bf16),
            pltpu.VMEM((NX, 2 * half_k, width), bf16),
            pltpu.VMEM((2, rows // 2, width), f32),
            pltpu.VMEM((2, rows, width), f32),
            pltpu.VMEM((3, rows, width), f32),
            pltpu.VMEM((rows, width), bf16),
            dma((4,)),
            dma((n, NX)),
            dma((n, 10)),
            dma((n, 4)),
            dma((n, 5)),
            dma((n, 2)),
            dma((n, 2)),
            dma((2, len(HALVES), nz)),
            dma((2, len(HALVES), nz)),
            dma((len(HALVES), nz)),
            dma((len(HALVES), nz)),
        ],
        compiler_params=pltpu.CompilerParams(collective_id=0, has_side_effects=True, vmem_limit_bytes=67043328),
    )(a_blk, b_blk)


def solution(mesh):
    nz, ny = mesh.shape["depth"], mesh.shape["col"]
    return jax.shard_map(
        functools.partial(local_product, nz, ny),
        mesh=mesh,
        in_specs=(P("row", "col"), P("row", "col")),
        out_specs=P(("row", "depth"), "col"),
        check_vma=False,
    )
```

time: 201 us -> 208 us (1.035)
  Pallas kernels: 198 us -> 204 us
    pallas_call x1, Pallas kernels: 198 us -> 204 us  [local_product(): pl.pallas_call(functools.partial(kernel, nz, ny), name='stationary_a', ou...]
where the time goes in v2:
time: 208 us
  Pallas kernels  204 us (98%)
  local copies, waits for them, and re-layouts  3.13 us (2%)
    pallas_call x1, Pallas kernels, local_product(): pl.pallas_call(functools.partial(kernel, nz, ny), name='stationary_a', ou...  204 us

profile of v2, /device:TPU:1, one launch (start us, length us, event | category | flops | bytes accessed | tf_op | source)
XLA Modules:
  0.0 207.5 jit_solution(5755682942571656160)
XLA Ops:
  0.0 204.4 %stationary_a.1 = bf16[256,4096]{1,0:T(8,128)(2,1)} custom-call(bf16[2048,4096]{1,0:T(8,128)(2,1)} %a_ref.1, bf16[2048,4096]{1,0:T(8,128)(2,1)} %b_ref.1), custom_call_target="tpu_custom_call" | custom-call | tf_op jit(solution)/shard_map/stationary_a/pallas_call | solution.py:267
  204.4 3.1 %copy.4 = bf16[256,4096]{1,0:T(8,128)(2,1)} copy(bf16[256,4096]{1,0:T(8,128)(2,1)} %stationary_a.1) | data formatting | bytes 4194304

commit v3 on v2

--- a/solution.py
+++ b/solution.py
@@ -9,12 +9,14 @@
 
 MESH = pl.DeviceIdType.MESH
 NX = 4
-PIECES = [(2, 0, 4), (2, 4, 4), (2, 8, 8), (1, 0, 8), (3, 0, 8), (1, 8, 8), (3, 8, 8), (0, 0, 16)]
-OPPOSITE = [0, 1, 2]
-HALVES = [(0, 8), (8, 8)]
+PIECES = [(2, 0, True), (1, 0, True), (3, 0, True), (2, 1, False), (1, 1, False), (3, 1, False),
+          (2, 2, False), (1, 2, False), (3, 2, False), (0, 3, False)]
+GROUPS = [(0, 4), (4, 4), (8, 8), (0, 16)]
+NG = 3
 SLOT = {2: 0, 1: 1, 3: 2, 0: 0}
-SCRIPT = """S2:0 S2:1 S2:2 G0 S1:3 S3:4 G1 L0 R0 L1 R1 O0 G2 C0a L2 R2 C0b O1 C1a S1:5 S3:6 G3 C1b G4 O2 C2a L3 R3 C2b L4 R4 O3 S0:7
-C3a G5 C3b O4 C4a G6 C4b M0 L5 R5 L6 R6 O5 C5a G7 C5b O6 C6a L7 R7 C6b M1 O7 C7a C7b F0 F1"""
+SCRIPT = """S0 G0 G1 G2 S1 L0 R0 O0 C0a L1 R1 C0b L2 R2 O1 C1a G3 O2 C1b G4 G5 C2a S2 L3 R3 C2b M0
+L4 R4 O3 C3a L5 R5 C3b O4 C4a O5 G6 C4b G7 G8 C5a S3 L6 R6 C5b M1
+L7 R7 O6 C6a L8 R8 C6b O7 C7a O8 G9 C7b C8a L9 C8b M2 R9 O9 C9a C9b F0 F1 F2"""
 
 
 def chunk_order(nz):
@@ -45,7 +47,7 @@
                                             device_id=device, device_id_type=MESH)
 
     sibling = dev(z, y, x, 1 - c)
-    left, right = dev(z, y, x - 1, c), dev(z, y, x + 1, c)
+    left, right, far = dev(z, y, x - 1, c), dev(z, y, x + 1, c), dev(z, y, x + 2, c)
 
     a_copies = [pltpu.make_async_copy(a_ref.at[pl.ds(m * mblk, mblk)], abuf.at[pl.ds(m * mblk, mblk)], a_sem.at[m])
                 for m in range(4)]
@@ -62,11 +64,15 @@
 
     t_me = (y - x + NX) % NX
 
+    def group_columns(s):
+        return pl.ds(GROUPS[s][0] * unit, GROUPS[s][1] * unit)
+
     def columns(n):
-        return pl.ds(PIECES[n][1] * unit, PIECES[n][2] * unit)
+        return group_columns(PIECES[n][1])
 
     def stage1(n, q, local, act):
-        t, first, wide = PIECES[n]
+        t = PIECES[n][0]
+        first, wide = GROUPS[PIECES[n][1]]
         cols = pl.ds(pl.multiple_of(z * width + first * unit, 4 * unit), wide * unit)
         src = b_ref.at[pl.ds(q * quarter, quarter), cols]
         dst = bbuf.at[t, pl.ds(pl.multiple_of(c * half_k + q * quarter, quarter), quarter), columns(n)]
@@ -107,24 +113,27 @@
         return remote(ref, ref, fw_send.at[n, k], b_recv.at[n, c * 5 + k], sibling)
 
     def to_side(n, which):
+        straight = PIECES[n][2]
         if which < 2:
             ref = part(n, c, 0)
         else:
-            q = (x + (3, 1)[which - 2]) % NX
+            q = x if straight else (x + (3, 1)[which - 2]) % NX
             size = quarter // 2
             start = c * half_k + q * quarter + (which - 2) * size
             ref = bbuf.at[PIECES[n][0], pl.ds(pl.multiple_of(start, size), size), columns(n)]
-        return remote(ref, ref, ag_send.at[n, which], b_recv.at[n, c * 5 + 1 + which], (right, left)[which % 2])
+        target = far if straight and which >= 2 else (right, left)[which % 2]
+        return remote(ref, ref, ag_send.at[n, which], b_recv.at[n, c * 5 + 1 + which], target)
 
     def pass_own(n):
         arrived(n, c, 0)
-        to_side(n, 0).start()
-        to_side(n, 1).start()
+        for which in (2, 3, 0, 1) if PIECES[n][2] else (0, 1):
+            to_side(n, which).start()
         to_sibling(n, 0).start()
 
     def pass_side(n, k):
         arrived(n, c, k)
-        to_side(n, k + 1).start()
+        if not PIECES[n][2]:
+            to_side(n, k + 1).start()
         to_sibling(n, k).start()
 
     def pass_far(n):
@@ -132,9 +141,9 @@
             arrived(n, c, k)
             to_sibling(n, k).start()
 
-    def opposite_copy(n, d):
-        return remote(pbuf.at[0, pl.ds(d * half, half), columns(n)], ro.at[d, :, columns(n)],
-                      op_send.at[n, d], op_recv.at[n, d], dev(z, y + 1 - 2 * d, x, c))
+    def opposite_copy(s, d):
+        return remote(pbuf.at[0, pl.ds(d * half, half), group_columns(s)], ro.at[d, :, group_columns(s)],
+                      op_send.at[s, d], op_recv.at[s, d], dev(z, y + 1 - 2 * d, x, c))
 
     def half_matmul(n, h):
         t = PIECES[n][0]
@@ -145,7 +154,7 @@
                 for cp in a_copies:
                     cp.wait()
             if t == 0:
-                for m in OPPOSITE:
+                for m in range(NG):
                     for d in (0, 1):
                         opposite_copy(m, d).wait_send()
 
@@ -157,27 +166,21 @@
 
         lax.fori_loop(2 * h, 2 * h + 2, body, 0)
         if t == 2:
-            opposite_copy(n, h).start()
+            opposite_copy(PIECES[n][1], h).start()
 
     def chunk_rows(r):
         zz = (z + r) % nz
         return pl.ds(pl.multiple_of(zz * chunk, chunk), chunk)
 
-    def half_columns(s):
-        return pl.ds(HALVES[s][0] * unit, HALVES[s][1] * unit)
-
     def neighbour_copy(d, s, r):
-        cr, cols = chunk_rows(r), half_columns(s)
+        cr, cols = chunk_rows(r), group_columns(s)
         return remote(pbuf.at[1 + d, cr, cols], rn.at[d, cr, cols], nb_send.at[d, s, r], nb_recv.at[d, s, r],
                       dev(z, y + 1 - 2 * d, x, c))
 
     def merge(s):
-        first, wide = HALVES[s]
-        cols = half_columns(s)
-        for n in OPPOSITE:
-            if first <= PIECES[n][1] < first + wide:
-                for d in (0, 1):
-                    opposite_copy(n, d).wait_recv()
+        cols = group_columns(s)
+        for d in (0, 1):
+            opposite_copy(s, d).wait_recv()
         for d in (0, 1):
             def body(m, carry):
                 r = pl.ds(pl.multiple_of(m * (half // 4), half // 4), half // 4)
@@ -191,10 +194,10 @@
                 neighbour_copy(d, s, r).start()
 
     def out_columns(zz, s):
-        return pl.ds(pl.multiple_of(zz * width + HALVES[s][0] * unit, 8 * unit), HALVES[s][1] * unit)
+        return pl.ds(pl.multiple_of(zz * width + GROUPS[s][0] * unit, 4 * unit), GROUPS[s][1] * unit)
 
     def out_copy(s, r):
-        src = obuf.at[chunk_rows(r), half_columns(s)]
+        src = obuf.at[chunk_rows(r), group_columns(s)]
         if r == 0:
             return pltpu.make_async_copy(src, o_ref.at[:, out_columns(z, s)], out_recv.at[s, 0])
         return remote(src, o_ref.at[:, out_columns(z, s)], out_send.at[s, r], out_recv.at[s, r], dev(z + r, y, x, c))
@@ -203,11 +206,11 @@
         if r == 0:
             out_copy(s, 0).wait()
         else:
-            remote(obuf.at[chunk_rows(r), half_columns(s)], o_ref.at[:, out_columns((z - r + nz) % nz, s)],
+            remote(obuf.at[chunk_rows(r), group_columns(s)], o_ref.at[:, out_columns((z - r + nz) % nz, s)],
                    out_send.at[s, r], out_recv.at[s, r], dev(z + r, y, x, c)).wait_recv()
 
     def finish(s):
-        cols = half_columns(s)
+        cols = group_columns(s)
         for r in order_z:
             for d in (0, 1):
                 neighbour_copy(d, s, r).wait_recv()
@@ -219,11 +222,11 @@
     for item in SCRIPT.split():
         op, rest = item[0], item[1:]
         if op == "S":
-            t, n = (int(v) for v in rest.split(":"))
-
-            @pl.when(t_me == t)
-            def _():
-                stage1_all(n, lambda cp: cp.start(), True)
+            for n in range(len(PIECES)):
+                if PIECES[n][1] == int(rest):
+                    @pl.when(t_me == PIECES[n][0])
+                    def _():
+                        stage1_all(n, lambda cp: cp.start(), True)
         elif op == "G":
             pass_own(int(rest))
         elif op == "L":
@@ -248,7 +251,7 @@
             to_side(n, which).wait_send()
         for k in range(5):
             to_sibling(n, k).wait_send()
-    for s in range(len(HALVES)):
+    for s in range(NG):
         for r in order_z:
             for d in (0, 1):
                 neighbour_copy(d, s, r).wait_send()
@@ -282,12 +285,12 @@
             dma((n, 10)),
             dma((n, 4)),
             dma((n, 5)),
-            dma((n, 2)),
-            dma((n, 2)),
-            dma((2, len(HALVES), nz)),
-            dma((2, len(HALVES), nz)),
-            dma((len(HALVES), nz)),
-            dma((len(HALVES), nz)),
+            dma((NG, 2)),
+            dma((NG, 2)),
+            dma((2, NG, nz)),
+            dma((2, NG, nz)),
+            dma((NG, nz)),
+            dma((NG, nz)),
         ],
         compiler_params=pltpu.CompilerParams(collective_id=0, has_side_effects=True, vmem_limit_bytes=67043328),
     )(a_blk, b_blk)

time: 208 us -> 227 us (1.091)
  the two profiles are of different devices: /device:TPU:1 before, /device:TPU:18 now
where the time goes in v3:
time: 227 us
  Pallas kernels  224 us (99%)
  local copies, waits for them, and re-layouts  3.13 us (1%)
    pallas_call x1, Pallas kernels, local_product(): pl.pallas_call(functools.partial(kernel, nz, ny), name='stationary_a', ou...  224 us

profile of v3, /device:TPU:18, one launch (start us, length us, event | category | flops | bytes accessed | tf_op | source)
XLA Modules:
  0.0 227.1 jit_solution(1594124798929482456)
XLA Ops:
  0.0 224.0 %stationary_a.1 = bf16[256,4096]{1,0:T(8,128)(2,1)} custom-call(bf16[2048,4096]{1,0:T(8,128)(2,1)} %a_ref.1, bf16[2048,4096]{1,0:T(8,128)(2,1)} %b_ref.1), custom_call_target="tpu_custom_call" | custom-call | tf_op jit(solution)/shard_map/stationary_a/pallas_call | solution.py:270
  224.0 3.1 %copy.4 = bf16[256,4096]{1,0:T(8,128)(2,1)} copy(bf16[256,4096]{1,0:T(8,128)(2,1)} %stationary_a.1) | data formatting | bytes 4194304

commit v4 on v3

--- a/solution.py
+++ b/solution.py
@@ -9,14 +9,14 @@
 
 MESH = pl.DeviceIdType.MESH
 NX = 4
-PIECES = [(2, 0, True), (1, 0, True), (3, 0, True), (2, 1, False), (1, 1, False), (3, 1, False),
-          (2, 2, False), (1, 2, False), (3, 2, False), (0, 3, False)]
+PIECES = [(2, 0, True), (1, 0, True), (3, 0, True), (2, 1, True), (1, 1, True), (3, 1, True),
+          (2, 2, True), (1, 2, True), (3, 2, True), (0, 3, True)]
 GROUPS = [(0, 4), (4, 4), (8, 8), (0, 16)]
 NG = 3
 SLOT = {2: 0, 1: 1, 3: 2, 0: 0}
-SCRIPT = """S0 G0 G1 G2 S1 L0 R0 O0 C0a L1 R1 C0b L2 R2 O1 C1a G3 O2 C1b G4 G5 C2a S2 L3 R3 C2b M0
-L4 R4 O3 C3a L5 R5 C3b O4 C4a O5 G6 C4b G7 G8 C5a S3 L6 R6 C5b M1
-L7 R7 O6 C6a L8 R8 C6b O7 C7a O8 G9 C7b C8a L9 C8b M2 R9 O9 C9a C9b F0 F1 F2"""
+SCRIPT = """S0 G0 G1 G2 S1 L0 R0 O0 C0a L1 R1 C0b O1 L2 R2 C1a O2 C1b G3 G4 G5 S2 C2a C2b M0
+L3 R3 O3 L4 R4 O4 C3a G6 G7 G8 S3 C3b L5 R5 O5 C4a C4b C5a C5b M1 G9 L6 R6 O6 C6a L7 R7 C6b O7 L8 R8 O8 C7a C7b C8a C8b M2
+L9 R9 O9 C9a C9b F0 F1 F2"""
 
 
 def chunk_order(nz):

time: 227 us -> 221 us (0.974)
  the two profiles are of different devices: /device:TPU:18 before, /device:TPU:30 now
where the time goes in v4:
time: 221 us
  Pallas kernels  217 us (98%)
  local copies, waits for them, and re-layouts  3.13 us (1%)
    pallas_call x1, Pallas kernels, local_product(): pl.pallas_call(functools.partial(kernel, nz, ny), name='stationary_a', ou...  217 us

profile of v4, /device:TPU:30, one launch (start us, length us, event | category | flops | bytes accessed | tf_op | source)
XLA Modules:
  0.0 220.5 jit_solution(7743655789052727507)
XLA Ops:
  0.0 217.4 %stationary_a.1 = bf16[256,4096]{1,0:T(8,128)(2,1)} custom-call(bf16[2048,4096]{1,0:T(8,128)(2,1)} %a_ref.1, bf16[2048,4096]{1,0:T(8,128)(2,1)} %b_ref.1), custom_call_target="tpu_custom_call" | custom-call | tf_op jit(solution)/shard_map/stationary_a/pallas_call | solution.py:270
  217.4 3.1 %copy.4 = bf16[256,4096]{1,0:T(8,128)(2,1)} copy(bf16[256,4096]{1,0:T(8,128)(2,1)} %stationary_a.1) | data formatting | bytes 4194304

commit v5 on v4

--- a/solution.py
+++ b/solution.py
@@ -9,13 +9,13 @@
 
 MESH = pl.DeviceIdType.MESH
 NX = 4
-PIECES = [(2, 0, True), (1, 0, True), (3, 0, True), (2, 1, True), (1, 1, True), (3, 1, True),
-          (2, 2, True), (1, 2, True), (3, 2, True), (0, 3, True)]
+PIECES = [(2, 0, True), (1, 0, True), (3, 0, True), (2, 1, True), (2, 2, True), (1, 1, True), (3, 1, True),
+          (1, 2, True), (3, 2, True), (0, 3, True)]
 GROUPS = [(0, 4), (4, 4), (8, 8), (0, 16)]
 NG = 3
 SLOT = {2: 0, 1: 1, 3: 2, 0: 0}
-SCRIPT = """S0 G0 G1 G2 S1 L0 R0 O0 C0a L1 R1 C0b O1 L2 R2 C1a O2 C1b G3 G4 G5 S2 C2a C2b M0
-L3 R3 O3 L4 R4 O4 C3a G6 G7 G8 S3 C3b L5 R5 O5 C4a C4b C5a C5b M1 G9 L6 R6 O6 C6a L7 R7 C6b O7 L8 R8 O8 C7a C7b C8a C8b M2
+SCRIPT = """S0 S1 G0 G1 G2 S2 S3 L0 R0 O0 C0a L1 R1 C0b O1 L2 R2 O2 C1a G3 C1b C2a G5 G6 C2b U0 M0
+L3 R3 O3 C3a G4 C3b L5 R5 O5 L6 R6 O6 G7 G8 C5a C5b L4 R4 O4 C4a C4b C6a C6b A1 G9 L7 R7 O7 C7a C7b L8 R8 O8 C8a C8b A2
 L9 R9 O9 C9a C9b F0 F1 F2"""
 
 
@@ -168,14 +168,19 @@
         if t == 2:
             opposite_copy(PIECES[n][1], h).start()
 
-    def chunk_rows(r):
-        zz = (z + r) % nz
+    def chunk_rows(zz):
         return pl.ds(pl.multiple_of(zz * chunk, chunk), chunk)
 
-    def neighbour_copy(d, s, r):
-        cr, cols = chunk_rows(r), group_columns(s)
-        return remote(pbuf.at[1 + d, cr, cols], rn.at[d, cr, cols], nb_send.at[d, s, r], nb_recv.at[d, s, r],
+    def neighbour_copy(d, s, zz):
+        cr, cols = chunk_rows(zz), group_columns(s)
+        return remote(pbuf.at[1 + d, cr, cols], rn.at[d, cr, cols], nb_send.at[d, s, zz], nb_recv.at[d, s, zz],
                       dev(z, y + 1 - 2 * d, x, c))
+
+    def send_half(s, merged):
+        nh = max(nz // 2, 1)
+        for j in range(nh):
+            for d in (0, 1):
+                neighbour_copy(d, s, ((d if merged else 1 - d) * nh + (z + j) % nh) % nz).start()
 
     def merge(s):
         cols = group_columns(s)
@@ -189,15 +194,17 @@
                 return carry
 
             lax.fori_loop(0, 4, body, 0)
+
+    def send_all(s):
         for r in order_z:
             for d in (0, 1):
-                neighbour_copy(d, s, r).start()
+                neighbour_copy(d, s, (z + r) % nz).start()
 
     def out_columns(zz, s):
         return pl.ds(pl.multiple_of(zz * width + GROUPS[s][0] * unit, 4 * unit), GROUPS[s][1] * unit)
 
     def out_copy(s, r):
-        src = obuf.at[chunk_rows(r), group_columns(s)]
+        src = obuf.at[chunk_rows((z + r) % nz), group_columns(s)]
         if r == 0:
             return pltpu.make_async_copy(src, o_ref.at[:, out_columns(z, s)], out_recv.at[s, 0])
         return remote(src, o_ref.at[:, out_columns(z, s)], out_send.at[s, r], out_recv.at[s, r], dev(z + r, y, x, c))
@@ -206,15 +213,15 @@
         if r == 0:
             out_copy(s, 0).wait()
         else:
-            remote(obuf.at[chunk_rows(r), group_columns(s)], o_ref.at[:, out_columns((z - r + nz) % nz, s)],
+            remote(obuf.at[chunk_rows((z + r) % nz), group_columns(s)], o_ref.at[:, out_columns((z - r + nz) % nz, s)],
                    out_send.at[s, r], out_recv.at[s, r], dev(z + r, y, x, c)).wait_recv()
 
     def finish(s):
         cols = group_columns(s)
         for r in order_z:
             for d in (0, 1):
-                neighbour_copy(d, s, r).wait_recv()
-            cr = chunk_rows(r)
+                neighbour_copy(d, s, (z + r) % nz).wait_recv()
+            cr = chunk_rows((z + r) % nz)
             total = pbuf[0, cr, cols] + rn[0, cr, cols] + rn[1, cr, cols]
             obuf[cr, cols] = total.astype(jnp.bfloat16)
             out_copy(s, r).start()
@@ -237,8 +244,14 @@
             pass_far(int(rest))
         elif op == "C":
             half_matmul(int(rest[0]), "ab".index(rest[1]))
+        elif op == "U":
+            send_half(int(rest), False)
         elif op == "M":
             merge(int(rest))
+            send_half(int(rest), True)
+        elif op == "A":
+            merge(int(rest))
+            send_all(int(rest))
         elif op == "F":
             finish(int(rest))
 
@@ -254,7 +267,7 @@
     for s in range(NG):
         for r in order_z:
             for d in (0, 1):
-                neighbour_copy(d, s, r).wait_send()
+                neighbour_copy(d, s, (z + r) % nz).wait_send()
             if r:
                 out_copy(s, r).wait_send()
             out_arrived(s, r)

time: 221 us -> 199 us (0.900)
  the two profiles are of different devices: /device:TPU:30 before, /device:TPU:1 now
where the time goes in v5:
time: 199 us; the launch traced here: 196 us
  Pallas kernels  193 us (97%)
  local copies, waits for them, and re-layouts  3.13 us (2%)
    pallas_call x1, Pallas kernels, local_product(): pl.pallas_call(functools.partial(kernel, nz, ny), name='stationary_a', ou...  193 us

profile of v5, /device:TPU:1, one launch (start us, length us, event | category | flops | bytes accessed | tf_op | source)
XLA Modules:
  0.0 196.3 jit_solution(14304221523234478660)
XLA Ops:
  0.0 193.1 %stationary_a.1 = bf16[256,4096]{1,0:T(8,128)(2,1)} custom-call(bf16[2048,4096]{1,0:T(8,128)(2,1)} %a_ref.1, bf16[2048,4096]{1,0:T(8,128)(2,1)} %b_ref.1), custom_call_target="tpu_custom_call" | custom-call | tf_op jit(solution)/shard_map/stationary_a/pallas_call | solution.py:283
  193.2 3.1 %copy.4 = bf16[256,4096]{1,0:T(8,128)(2,1)} copy(bf16[256,4096]{1,0:T(8,128)(2,1)} %stationary_a.1) | data formatting | bytes 4194304

commit v6 on v5

--- a/solution.py
+++ b/solution.py
@@ -14,9 +14,9 @@
 GROUPS = [(0, 4), (4, 4), (8, 8), (0, 16)]
 NG = 3
 SLOT = {2: 0, 1: 1, 3: 2, 0: 0}
-SCRIPT = """S0 S1 G0 G1 G2 S2 S3 L0 R0 O0 C0a L1 R1 C0b O1 L2 R2 O2 C1a G3 C1b C2a G5 G6 C2b U0 M0
-L3 R3 O3 C3a G4 C3b L5 R5 O5 L6 R6 O6 G7 G8 C5a C5b L4 R4 O4 C4a C4b C6a C6b A1 G9 L7 R7 O7 C7a C7b L8 R8 O8 C8a C8b A2
-L9 R9 O9 C9a C9b F0 F1 F2"""
+SCRIPT = """X0 S0 X1 X2 X3 S3 G0 S1 S2 G3 X5 X6 X4 X7 X8 X9 L0 R0 O0 C0a G1 G2 C0b S5 S6 S4 L3 R3 O3 C3a L1 R1 C3b O1 L2 R2 O2
+C1a S7 S8 C1b C2a S9 C2b U0 M0 G4 G5 G6 L4 R4 O4 C4a G7 G8 C4b L5 R5 O5 C5a G9 C5b L6 R6 O6 C6a C6b A1
+L7 R7 O7 C7a C7b L8 R8 O8 C8a C8b A2 L9 R9 O9 C9a C9b W F0 F1 V F2"""
 
 
 def chunk_order(nz):
@@ -70,31 +70,29 @@
     def columns(n):
         return group_columns(PIECES[n][1])
 
-    def stage1(n, q, local, act):
-        t = PIECES[n][0]
-        first, wide = GROUPS[PIECES[n][1]]
+    def stage1(n, d):
+        t, group, _ = PIECES[n]
+        first, wide = GROUPS[group]
+        q = (x + d) % NX
         cols = pl.ds(pl.multiple_of(z * width + first * unit, 4 * unit), wide * unit)
-        src = b_ref.at[pl.ds(q * quarter, quarter), cols]
+        src = b_ref.at[pl.ds(pl.multiple_of(q * quarter, quarter), quarter), cols]
         dst = bbuf.at[t, pl.ds(pl.multiple_of(c * half_k + q * quarter, quarter), quarter), columns(n)]
-        sem = b_recv.at[n, c * 5]
-        if local:
-            act(pltpu.make_async_copy(src, dst, sem))
-        else:
-            act(remote(src, dst, s1_send.at[n, q], sem, dev(z, x, q, c)))
-
-    def stage1_all(n, act, with_local):
-        for q in range(NX):
-            if PIECES[n][0]:
-                stage1(n, q, False, act)
-            else:
-                @pl.when(x != q)
-                def _():
-                    stage1(n, q, False, act)
-
-                if with_local:
-                    @pl.when(x == q)
-                    def _():
-                        stage1(n, q, True, act)
+        if t == 0 and d == 0:
+            return pltpu.make_async_copy(src, dst, b_recv.at[n, c * 5])
+        return remote(src, dst, s1_send.at[n, d], b_recv.at[n, c * 5], dev(z, x, q, c))
+
+    def stage1_start(n, ds):
+        @pl.when(t_me == PIECES[n][0])
+        def _():
+            for d in ds:
+                stage1(n, d).start()
+
+    def stage1_sent(n):
+        @pl.when(t_me == PIECES[n][0])
+        def _():
+            for d in range(NX):
+                if PIECES[n][0] or d:
+                    stage1(n, d).wait_send()
 
     def part(n, lane, k):
         q = (x + (0, 3, 1, 2, 2)[k]) % NX
@@ -141,12 +139,13 @@
             arrived(n, c, k)
             to_sibling(n, k).start()
 
-    def opposite_copy(s, d):
-        return remote(pbuf.at[0, pl.ds(d * half, half), group_columns(s)], ro.at[d, :, group_columns(s)],
-                      op_send.at[s, d], op_recv.at[s, d], dev(z, y + 1 - 2 * d, x, c))
+    def opposite_copy(s, d, h):
+        src = pbuf.at[0, pl.ds(pl.multiple_of(d * half + h * mblk, mblk), mblk), group_columns(s)]
+        return remote(src, ro.at[d, pl.ds(h * mblk, mblk), group_columns(s)], op_send.at[s, d, h], op_recv.at[s, d, h],
+                      dev(z, y + 1 - 2 * d, x, c))
 
     def half_matmul(n, h):
-        t = PIECES[n][0]
+        t, group, _ = PIECES[n]
         if h == 0:
             for k in range(5):
                 arrived(n, 1 - c, k)
@@ -156,17 +155,18 @@
             if t == 0:
                 for m in range(NG):
                     for d in (0, 1):
-                        opposite_copy(m, d).wait_send()
-
-        def body(m, carry):
-            r = pl.ds(pl.multiple_of(m * mblk, mblk), mblk)
+                        for hh in (0, 1):
+                            opposite_copy(m, d, hh).wait_send()
+
+        def body(d, carry):
+            r = pl.ds(pl.multiple_of(d * half + h * mblk, mblk), mblk)
             pbuf[SLOT[t], r, columns(n)] = jnp.dot(abuf[r, :], bbuf[t, :, columns(n)],
                                                    preferred_element_type=jnp.float32)
+            if t == 2:
+                opposite_copy(group, d, h).start()
             return carry
 
-        lax.fori_loop(2 * h, 2 * h + 2, body, 0)
-        if t == 2:
-            opposite_copy(PIECES[n][1], h).start()
+        lax.fori_loop(0, 2, body, 0)
 
     def chunk_rows(zz):
         return pl.ds(pl.multiple_of(zz * chunk, chunk), chunk)
@@ -185,7 +185,8 @@
     def merge(s):
         cols = group_columns(s)
         for d in (0, 1):
-            opposite_copy(s, d).wait_recv()
+            for h in (0, 1):
+                opposite_copy(s, d, h).wait_recv()
         for d in (0, 1):
             def body(m, carry):
                 r = pl.ds(pl.multiple_of(m * (half // 4), half // 4), half // 4)
@@ -226,14 +227,20 @@
             obuf[cr, cols] = total.astype(jnp.bfloat16)
             out_copy(s, r).start()
 
+    def out_done(s):
+        for r in order_z:
+            for d in (0, 1):
+                neighbour_copy(d, s, (z + r) % nz).wait_send()
+            if r:
+                out_copy(s, r).wait_send()
+            out_arrived(s, r)
+
     for item in SCRIPT.split():
         op, rest = item[0], item[1:]
-        if op == "S":
-            for n in range(len(PIECES)):
-                if PIECES[n][1] == int(rest):
-                    @pl.when(t_me == PIECES[n][0])
-                    def _():
-                        stage1_all(n, lambda cp: cp.start(), True)
+        if op == "X":
+            stage1_start(int(rest), (0,))
+        elif op == "S":
+            stage1_start(int(rest), (2, 1, 3))
         elif op == "G":
             pass_own(int(rest))
         elif op == "L":
@@ -254,23 +261,18 @@
             send_all(int(rest))
         elif op == "F":
             finish(int(rest))
-
-    for n in range(len(PIECES)):
-        @pl.when(t_me == PIECES[n][0])
-        def _():
-            stage1_all(n, lambda cp: cp.wait_send(), False)
-
-        for which in range(4):
-            to_side(n, which).wait_send()
-        for k in range(5):
-            to_sibling(n, k).wait_send()
-    for s in range(NG):
-        for r in order_z:
-            for d in (0, 1):
-                neighbour_copy(d, s, (z + r) % nz).wait_send()
-            if r:
-                out_copy(s, r).wait_send()
-            out_arrived(s, r)
+        elif op == "W":
+            for n in range(len(PIECES)):
+                stage1_sent(n)
+                for which in range(4):
+                    to_side(n, which).wait_send()
+                for k in range(5):
+                    to_sibling(n, k).wait_send()
+        elif op == "V":
+            for s in range(NG - 1):
+                out_done(s)
+
+    out_done(NG - 1)
 
 
 def local_product(nz, ny, a_blk, b_blk):
@@ -298,8 +300,8 @@
             dma((n, 10)),
             dma((n, 4)),
             dma((n, 5)),
-            dma((NG, 2)),
-            dma((NG, 2)),
+            dma((NG, 2, 2)),
+            dma((NG, 2, 2)),
             dma((2, NG, nz)),
             dma((2, NG, nz)),
             dma((NG, nz)),

time: 199 us -> 216 us (1.085)
  the two profiles are of different devices: /device:TPU:1 before, /device:TPU:3 now
where the time goes in v6:
time: 216 us; the launch traced here: 215 us
  Pallas kernels  212 us (98%)
  local copies, waits for them, and re-layouts  3.13 us (1%)
    pallas_call x1, Pallas kernels, local_product(): pl.pallas_call(functools.partial(kernel, nz, ny), name='stationary_a', ou...  212 us

profile of v6, /device:TPU:3, one launch (start us, length us, event | category | flops | bytes accessed | tf_op | source)
XLA Modules:
  0.0 215.4 jit_solution(68806341561688993)
XLA Ops:
  0.0 212.3 %stationary_a.1 = bf16[256,4096]{1,0:T(8,128)(2,1)} custom-call(bf16[2048,4096]{1,0:T(8,128)(2,1)} %a_ref.1, bf16[2048,4096]{1,0:T(8,128)(2,1)} %b_ref.1), custom_call_target="tpu_custom_call" | custom-call | tf_op jit(solution)/shard_map/stationary_a/pallas_call | solution.py:285
  212.3 3.1 %copy.4 = bf16[256,4096]{1,0:T(8,128)(2,1)} copy(bf16[256,4096]{1,0:T(8,128)(2,1)} %stationary_a.1) | data formatting | bytes 4194304

commit v7 on v6

--- a/solution.py
+++ b/solution.py
@@ -9,14 +9,14 @@
 
 MESH = pl.DeviceIdType.MESH
 NX = 4
-PIECES = [(2, 0, True), (1, 0, True), (3, 0, True), (2, 1, True), (2, 2, True), (1, 1, True), (3, 1, True),
+PIECES = [(2, 0, True), (2, 1, True), (2, 2, True), (1, 0, True), (3, 0, True), (1, 1, True), (3, 1, True),
           (1, 2, True), (3, 2, True), (0, 3, True)]
 GROUPS = [(0, 4), (4, 4), (8, 8), (0, 16)]
 NG = 3
 SLOT = {2: 0, 1: 1, 3: 2, 0: 0}
-SCRIPT = """X0 S0 X1 X2 X3 S3 G0 S1 S2 G3 X5 X6 X4 X7 X8 X9 L0 R0 O0 C0a G1 G2 C0b S5 S6 S4 L3 R3 O3 C3a L1 R1 C3b O1 L2 R2 O2
-C1a S7 S8 C1b C2a S9 C2b U0 M0 G4 G5 G6 L4 R4 O4 C4a G7 G8 C4b L5 R5 O5 C5a G9 C5b L6 R6 O6 C6a C6b A1
-L7 R7 O7 C7a C7b L8 R8 O8 C8a C8b A2 L9 R9 O9 C9a C9b W F0 F1 V F2"""
+SCRIPT = """P0 P3 P4 P1 P5 P6 G0 P2 P7 P8 P9 G1 L0 R0 O0 C0a C0b G2 G3 G4 L1 R1 O1 C1a C1b G5 G6 L2 R2 O2 C2a C2b G9
+L3 R3 O3 C3a L4 R4 O4 C3b C4a C4b A0 G7 G8 L5 R5 O5 C5a L6 R6 O6 C5b C6a C6b A1 L9 R9 O9 C9a C9b F0
+L7 R7 O7 C7a L8 R8 O8 C7b C8a C8b A2 W F1 F2 V"""
 
 
 def chunk_order(nz):
@@ -237,10 +237,8 @@
 
     for item in SCRIPT.split():
         op, rest = item[0], item[1:]
-        if op == "X":
-            stage1_start(int(rest), (0,))
-        elif op == "S":
-            stage1_start(int(rest), (2, 1, 3))
+        if op == "P":
+            stage1_start(int(rest), (0, 2, 1, 3))
         elif op == "G":
             pass_own(int(rest))
         elif op == "L":

time: 216 us -> 195 us (0.903)
  the two profiles are of different devices: /device:TPU:3 before, /device:TPU:1 now
where the time goes in v7:
time: 195 us; the launch traced here: 194 us
  Pallas kernels  191 us (98%)
  local copies, waits for them, and re-layouts  3.13 us (2%)
    pallas_call x1, Pallas kernels, local_product(): pl.pallas_call(functools.partial(kernel, nz, ny), name='stationary_a', ou...  191 us

profile of v7, /device:TPU:1, one launch (start us, length us, event | category | flops | bytes accessed | tf_op | source)
XLA Modules:
  0.0 194.2 jit_solution(4056873212683052667)
XLA Ops:
  0.0 191.1 %stationary_a.1 = bf16[256,4096]{1,0:T(8,128)(2,1)} custom-call(bf16[2048,4096]{1,0:T(8,128)(2,1)} %a_ref.1, bf16[2048,4096]{1,0:T(8,128)(2,1)} %b_ref.1), custom_call_target="tpu_custom_call" | custom-call | tf_op jit(solution)/shard_map/stationary_a/pallas_call | solution.py:283
  191.1 3.1 %copy.4 = bf16[256,4096]{1,0:T(8,128)(2,1)} copy(bf16[256,4096]{1,0:T(8,128)(2,1)} %stationary_a.1) | data formatting | bytes 4194304

commit v8 on v7

--- a/solution.py
+++ b/solution.py
@@ -10,13 +10,13 @@
 MESH = pl.DeviceIdType.MESH
 NX = 4
 PIECES = [(2, 0, True), (2, 1, True), (2, 2, True), (1, 0, True), (3, 0, True), (1, 1, True), (3, 1, True),
-          (1, 2, True), (3, 2, True), (0, 3, True)]
-GROUPS = [(0, 4), (4, 4), (8, 8), (0, 16)]
+          (1, 2, True), (3, 2, True), (0, 3, True), (0, 2, True)]
+GROUPS = [(0, 4), (4, 4), (8, 8), (0, 8)]
 NG = 3
 SLOT = {2: 0, 1: 1, 3: 2, 0: 0}
-SCRIPT = """P0 P3 P4 P1 P5 P6 G0 P2 P7 P8 P9 G1 L0 R0 O0 C0a C0b G2 G3 G4 L1 R1 O1 C1a C1b G5 G6 L2 R2 O2 C2a C2b G9
-L3 R3 O3 C3a L4 R4 O4 C3b C4a C4b A0 G7 G8 L5 R5 O5 C5a L6 R6 O6 C5b C6a C6b A1 L9 R9 O9 C9a C9b F0
-L7 R7 O7 C7a L8 R8 O8 C7b C8a C8b A2 W F1 F2 V"""
+SCRIPT = """P0 P3 P4 P1 P5 P6 G0 P2 G1 L0 R0 O0 C0a G2 C0b P7 P8 G3 G4 L1 R1 O1 C1a C1b G5 G6 P9 P10 L2 R2 O2 C2a C2b
+L3 R3 O3 C3a L4 R4 O4 C3b C4a C4b A0 G9 G7 G8 L5 R5 O5 C5a L6 R6 O6 C5b C6a C6b A1 G10 L9 R9 O9 C9a C9b F0
+L7 R7 O7 C7a L8 R8 O8 C7b C8a C8b A2 F1 L10 R10 O10 C10a C10b W F2 V"""
 
 
 def chunk_order(nz):
@@ -153,7 +153,7 @@
                 for cp in a_copies:
                     cp.wait()
             if t == 0:
-                for m in range(NG):
+                for m in (0, 1) if group == 3 else (2,):
                     for d in (0, 1):
                         for hh in (0, 1):
                             opposite_copy(m, d, hh).wait_send()
@@ -248,7 +248,7 @@
         elif op == "O":
             pass_far(int(rest))
         elif op == "C":
-            half_matmul(int(rest[0]), "ab".index(rest[1]))
+            half_matmul(int(rest[:-1]), "ab".index(rest[-1]))
         elif op == "U":
             send_half(int(rest), False)
         elif op == "M":

time: 195 us -> 189 us (0.969)
  Pallas kernels: 191 us -> 185 us
    pallas_call x1, Pallas kernels: 191 us -> 185 us  [local_product(): pl.pallas_call(functools.partial(kernel, nz, ny), name='stationary_a', ou...]
where the time goes in v8:
time: 189 us; the launch traced here: 188 us
  Pallas kernels  185 us (98%)
  local copies, waits for them, and re-layouts  3.13 us (2%)
    pallas_call x1, Pallas kernels, local_product(): pl.pallas_call(functools.partial(kernel, nz, ny), name='stationary_a', ou...  185 us

profile of v8, /device:TPU:1, one launch (start us, length us, event | category | flops | bytes accessed | tf_op | source)
XLA Modules:
  0.0 187.8 jit_solution(11341704768951775319)
XLA Ops:
  0.0 184.6 %stationary_a.1 = bf16[256,4096]{1,0:T(8,128)(2,1)} custom-call(bf16[2048,4096]{1,0:T(8,128)(2,1)} %a_ref.1, bf16[2048,4096]{1,0:T(8,128)(2,1)} %b_ref.1), custom_call_target="tpu_custom_call" | custom-call | tf_op jit(solution)/shard_map/stationary_a/pallas_call | solution.py:283
  184.7 3.1 %copy.4 = bf16[256,4096]{1,0:T(8,128)(2,1)} copy(bf16[256,4096]{1,0:T(8,128)(2,1)} %stationary_a.1) | data formatting | bytes 4194304

commit v9 on v8

v9 whole, which is shorter than its diff:
```python
import functools

import jax
import jax.numpy as jnp
from jax import lax
from jax.experimental import pallas as pl
from jax.experimental.pallas import tpu as pltpu
from jax.sharding import PartitionSpec as P

MESH = pl.DeviceIdType.MESH
NX = 4
PIECES = [(2, 0), (2, 1), (2, 2), (1, 0), (3, 0), (1, 1), (3, 1), (1, 2), (3, 2), (0, 3), (0, 2)]
GROUPS = [(0, 4), (4, 4), (8, 8), (0, 8)]
NG = 3
SLOT = {2: 0, 1: 1, 3: 2, 0: 0}
SCRIPT = """P0 P3 P4 P1 P5 P6 G0 P2 G1 L0 R0 O0 C0a C0b G2 P7 P8 G3 G4 L1 R1 O1 C1a C1b G5 G6 P9 P10 L2 R2 O2 C2a C2b
L3 R3 O3 C3a L4 R4 O4 C3b C4a C4b A0 G9 G7 G8 L5 R5 O5 C5a L6 R6 O6 C5b C6a C6b A1 G10 L9 R9 O9 C9a C9b F0
L7 R7 O7 C7a L8 R8 O8 C7b C8a C8b A2 F1 L10 R10 O10 C10a C10b W F2"""


def chunk_order(nz):
    return sorted(range(nz), key=lambda r: -min(r, nz - r))


def kernel(nz, ny, a_ref, b_ref, o_ref, abuf, bbuf, ro, rn, pbuf, obuf,
           a_sem, b_send, b_recv, s_recv, op_send, op_recv, nb_send, nb_recv, out_send, out_recv, own_sem):
    z = lax.axis_index("depth")
    y = lax.axis_index("col")
    i = lax.axis_index("row")
    x, c = i // 2, i % 2
    rows, depth_k = abuf.shape
    half_k = depth_k // 2
    quarter = half_k // NX
    width = depth_k // nz
    unit = width // 16
    chunk = rows // nz
    mblk = rows // 4
    half = rows // 2
    order_z = chunk_order(nz)

    def dev(zz, yy, xx, cc):
        return ((zz + nz) % nz, (yy + ny) % ny, 2 * ((xx + NX) % NX) + cc)

    def remote(src, dst, send_sem, recv_sem, device):
        return pltpu.make_async_remote_copy(src_ref=src, dst_ref=dst, send_sem=send_sem, recv_sem=recv_sem,
                                            device_id=device, device_id_type=MESH)

    sibling = dev(z, y, x, 1 - c)
    left, right, far = dev(z, y, x - 1, c), dev(z, y, x + 1, c), dev(z, y, x + 2, c)

    a_copies = [pltpu.make_async_copy(a_ref.at[pl.ds(m * mblk, mblk)], abuf.at[pl.ds(m * mblk, mblk)], a_sem)
                for m in range(4)]
    for cp in a_copies:
        cp.start()

    barrier = pltpu.get_barrier_semaphore()
    partners = [sibling]
    partners += [dev(z, y + dy, x + dx, c) for dy in range(ny) for dx in range(NX) if dx or dy]
    partners += [dev(z + r, y, x, c) for r in range(1, nz)]
    for p in partners:
        pl.semaphore_signal(barrier, inc=1, device_id=p, device_id_type=MESH)
    pl.semaphore_wait(barrier, len(partners))

    t_me = (y - x + NX) % NX

    def group_columns(s):
        return pl.ds(GROUPS[s][0] * unit, GROUPS[s][1] * unit)

    def columns(n):
        return group_columns(PIECES[n][1])

    def stage1(n, d):
        t, group = PIECES[n]
        first, wide = GROUPS[group]
        q = (x + d) % NX
        cols = pl.ds(pl.multiple_of(z * width + first * unit, 4 * unit), wide * unit)
        src = b_ref.at[pl.ds(pl.multiple_of(q * quarter, quarter), quarter), cols]
        dst = bbuf.at[t, pl.ds(pl.multiple_of(c * half_k + q * quarter, quarter), quarter), columns(n)]
        if t == 0 and d == 0:
            return pltpu.make_async_copy(src, dst, b_recv.at[n, 0])
        return remote(src, dst, b_send, b_recv.at[n, 0], dev(z, x, q, c))

    def stage1_start(n, ds):
        @pl.when(t_me == PIECES[n][0])
        def _():
            for d in ds:
                stage1(n, d).start()

    def part(n, k):
        q = (x + (0, 3, 1, 2)[k]) % NX
        start = c * half_k + q * quarter
        return bbuf.at[PIECES[n][0], pl.ds(pl.multiple_of(start, quarter), quarter), columns(n)]

    def lane(n, cc):
        return bbuf.at[PIECES[n][0], pl.ds(pl.multiple_of(cc * half_k, half_k), half_k), columns(n)]

    def arrived(n, k):
        ref = part(n, k)
        remote(ref, ref, b_send, b_recv.at[n, k], sibling).wait_recv()

    def to_sibling(n, k):
        ref = part(n, k)
        remote(ref, ref, b_send, s_recv.at[n], sibling).start()

    def pass_own(n):
        arrived(n, 0)
        ref = part(n, 0)
        for k, target in ((3, far), (1, right), (2, left)):
            remote(ref, ref, b_send, b_recv.at[n, k], target).start()
        to_sibling(n, 0)

    def pass_on(n, k):
        arrived(n, k)
        to_sibling(n, k)

    def group_columns(s):
        return pl.ds(GROUPS[s][0] * unit, GROUPS[s][1] * unit)

    def opposite_copy(s, d, h):
        src = pbuf.at[0, pl.ds(pl.multiple_of(d * half + h * mblk, mblk), mblk), group_columns(s)]
        return remote(src, ro.at[d, pl.ds(h * mblk, mblk), group_columns(s)], op_send.at[s], op_recv.at[s, d],
                      dev(z, y + 1 - 2 * d, x, c))

    def half_matmul(n, h):
        t, group = PIECES[n]
        if h == 0:
            ref = lane(n, 1 - c)
            remote(ref, ref, b_send, s_recv.at[n], sibling).wait_recv()
            if n == 0:
                pltpu.make_async_copy(abuf, abuf, a_sem).wait()
            if t == 0:
                for m in (0, 1) if group == 3 else (2,):
                    ref = pbuf.at[0, :, group_columns(m)]
                    remote(ref, ref, op_send.at[m], op_recv.at[m, 0], sibling).wait_send()

        def body(d, carry):
            r = pl.ds(pl.multiple_of(d * half + h * mblk, mblk), mblk)
            pbuf[SLOT[t], r, columns(n)] = jnp.dot(abuf[r, :], bbuf[t, :, columns(n)],
                                                   preferred_element_type=jnp.float32)
            if t == 2:
                opposite_copy(group, d, h).start()
            return carry

        lax.fori_loop(0, 2, body, 0)

    def chunk_rows(zz):
        return pl.ds(pl.multiple_of(zz * chunk, chunk), chunk)

    def neighbour_copy(d, s, zz):
        cr, cols = chunk_rows(zz), group_columns(s)
        return remote(pbuf.at[1 + d, cr, cols], rn.at[d, cr, cols], nb_send, nb_recv.at[d, s, zz],
                      dev(z, y + 1 - 2 * d, x, c))

    def send_half(s, merged):
        nh = max(nz // 2, 1)
        for j in range(nh):
            for d in (0, 1):
                neighbour_copy(d, s, ((d if merged else 1 - d) * nh + (z + j) % nh) % nz).start()

    def merge(s):
        cols = group_columns(s)
        for d in (0, 1):
            ref = ro.at[d, :, group_columns(s)]
            remote(ref, ref, op_send.at[s], op_recv.at[s, d], sibling).wait_recv()
        for d in (0, 1):
            def body(m, carry):
                r = pl.ds(pl.multiple_of(m * (half // 4), half // 4), half // 4)
                rp = pl.ds(pl.multiple_of(d * half + m * (half // 4), half // 4), half // 4)
                pbuf[1 + d, rp, cols] = pbuf[1 + d, rp, cols] + ro[d, r, cols]
                return carry

            lax.fori_loop(0, 4, body, 0)

    def send_all(s):
        for r in order_z:
            for d in (0, 1):
                neighbour_copy(d, s, (z + r) % nz).start()

    def out_columns(zz, s):
        return pl.ds(pl.multiple_of(zz * width + GROUPS[s][0] * unit, 4 * unit), GROUPS[s][1] * unit)

    def out_copy(s, r):
        src = obuf.at[chunk_rows((z + r) % nz), group_columns(s)]
        dst = o_ref.at[:, out_columns(z, s)]
        if r == 0:
            return pltpu.make_async_copy(src, dst, own_sem.at[s])
        return remote(src, dst, out_send, out_recv, dev(z + r, y, x, c))

    def finish(s):
        cols = group_columns(s)
        for r in order_z:
            for d in (0, 1):
                neighbour_copy(d, s, (z + r) % nz).wait_recv()
            cr = chunk_rows((z + r) % nz)
            total = pbuf[0, cr, cols] + rn[0, cr, cols] + rn[1, cr, cols]
            obuf[cr, cols] = total.astype(jnp.bfloat16)
            out_copy(s, r).start()

    for item in SCRIPT.split():
        op, rest = item[0], item[1:]
        if op == "P":
            stage1_start(int(rest), (0, 2, 1, 3))
        elif op == "G":
            pass_own(int(rest))
        elif op == "L":
            pass_on(int(rest), 1)
        elif op == "R":
            pass_on(int(rest), 2)
        elif op == "O":
            pass_on(int(rest), 3)
        elif op == "C":
            half_matmul(int(rest[:-1]), "ab".index(rest[-1]))
        elif op == "U":
            send_half(int(rest), False)
        elif op == "M":
            merge(int(rest))
            send_half(int(rest), True)
        elif op == "A":
            merge(int(rest))
            send_all(int(rest))
        elif op == "F":
            finish(int(rest))
        elif op == "W":
            @pl.when(t_me != 0)
            def _():
                remote(bbuf, bbuf, b_send, out_recv, sibling).wait_send()

            @pl.when(t_me == 0)
            def _():
                ref = bbuf.at[:, pl.ds(0, 2 * half_k - quarter // NX)]
                remote(ref, ref, b_send, out_recv, sibling).wait_send()

    remote(rn, rn, nb_send, out_recv, sibling).wait_send()
    for s in range(NG):
        out_copy(s, 0).wait()
    sent = obuf.at[pl.ds(0, rows - chunk)]
    remote(sent, sent, out_send, out_recv, sibling).wait_send()
    got = o_ref.at[pl.ds(0, chunk - chunk // nz)]
    remote(got, got, out_send, out_recv, sibling).wait_recv()


COPIES = 4


def copy_kernel(src_ref, dst_ref, buf, in_sem, out_sem):
    n = buf.shape[0] // COPIES
    blocks = [pl.ds(m * n, n) for m in range(COPIES)]
    ins = [pltpu.make_async_copy(src_ref.at[b], buf.at[b], in_sem.at[m]) for m, b in enumerate(blocks)]
    outs = [pltpu.make_async_copy(buf.at[b], dst_ref.at[b], out_sem.at[m]) for m, b in enumerate(blocks)]
    for cp in ins:
        cp.start()
    for cp_in, cp_out in zip(ins, outs):
        cp_in.wait()
        cp_out.start()
    for cp in outs:
        cp.wait()


def copy_out(c_rows):
    return pl.pallas_call(
        copy_kernel,
        name="copy_out",
        out_shape=jax.ShapeDtypeStruct(c_rows.shape, c_rows.dtype),
        in_specs=[pl.BlockSpec(memory_space=pl.ANY)],
        out_specs=pl.BlockSpec(memory_space=pl.ANY),
        scratch_shapes=[pltpu.VMEM(c_rows.shape, c_rows.dtype), pltpu.SemaphoreType.DMA((COPIES,)),
                        pltpu.SemaphoreType.DMA((COPIES,))],
    )(c_rows)


def local_product(nz, ny, a_blk, b_blk):
    rows, depth_k = a_blk.shape
    half_k = b_blk.shape[0]
    width = depth_k // nz
    f32, bf16 = jnp.float32, jnp.bfloat16
    dma = pltpu.SemaphoreType.DMA
    n = len(PIECES)
    return copy_out(pl.pallas_call(
        functools.partial(kernel, nz, ny),
        name="stationary_a",
        out_shape=jax.ShapeDtypeStruct((rows // nz, depth_k), bf16),
        in_specs=[pl.BlockSpec(memory_space=pl.ANY)] * 2,
        out_specs=pl.BlockSpec(memory_space=pl.ANY),
        scratch_shapes=[
            pltpu.VMEM((rows, depth_k), bf16),
            pltpu.VMEM((NX, 2 * half_k, width), bf16),
            pltpu.VMEM((2, rows // 2, width), f32),
            pltpu.VMEM((2, rows, width), f32),
            pltpu.VMEM((3, rows, width), f32),
            pltpu.VMEM((rows, width), bf16),
            dma,
            dma,
            dma((n, 4)),
            dma((n,)),
            dma((NG,)),
            dma((NG, 2)),
            dma,
            dma((2, NG, nz)),
            dma,
            dma,
            dma((NG,)),
        ],
        compiler_params=pltpu.CompilerParams(collective_id=0, has_side_effects=True, vmem_limit_bytes=67043328),
    )(a_blk, b_blk))


def solution(mesh):
    nz, ny = mesh.shape["depth"], mesh.shape["col"]
    return jax.shard_map(
        functools.partial(local_product, nz, ny),
        mesh=mesh,
        in_specs=(P("row", "col"), P("row", "col")),
        out_specs=P(("row", "depth"), "col"),
        check_vma=False,
    )
```

time: 189 us -> 190 us (level)
  Pallas kernels: 185 us -> 190 us
  local copies, waits for them, and re-layouts: 3.13 us -> 0 us
    unnamed x1 -> x0, local copies, waits for them, and re-layouts: 3.13 us -> none
    pallas_call x1, Pallas kernels: 185 us -> 187 us  [local_product(): pl.pallas_call(functools.partial(kernel, nz, ny), name='stationary_a', ou...]
    pallas_call x0 -> x1, Pallas kernels: none -> 2.42 us  [copy_out(): pl.pallas_call(copy_kernel, name='copy_out', out_shape=jax.ShapeDtypeStru...]
where the time goes in v9:
time: 190 us
  Pallas kernels  190 us (100%)
    pallas_call x1, Pallas kernels, local_product(): pl.pallas_call(functools.partial(kernel, nz, ny), name='stationary_a', ou...  187 us

profile of v9, /device:TPU:1, one launch (start us, length us, event | category | flops | bytes accessed | tf_op | source)
XLA Modules:
  0.0 189.8 jit_solution(1413448563680232410)
XLA Ops:
  0.0 187.2 %stationary_a.1.src_ref = bf16[256,4096]{1,0:T(8,128)(2,1)} custom-call(bf16[2048,4096]{1,0:T(8,128)(2,1)} %a_ref.1, bf16[2048,4096]{1,0:T(8,128)(2,1)} %b_ref.1), custom_call_target="tpu_custom_call" | custom-call | tf_op jit(solution)/shard_map/stationary_a/pallas_call | solution.py:278
  187.2 2.4 %copy_out.1 = bf16[256,4096]{1,0:T(8,128)(2,1)} custom-call(bf16[256,4096]{1,0:T(8,128)(2,1)} %stationary_a.1.src_ref), custom_call_target="tpu_custom_call" | custom-call | tf_op jit(solution)/shard_map/copy_out/pallas_call | solution.py:260

commit v10 on v9

--- a/solution.py
+++ b/solution.py
@@ -13,8 +13,8 @@
 GROUPS = [(0, 4), (4, 4), (8, 8), (0, 8)]
 NG = 3
 SLOT = {2: 0, 1: 1, 3: 2, 0: 0}
-SCRIPT = """P0 P3 P4 P1 P5 P6 G0 P2 G1 L0 R0 O0 C0a C0b G2 P7 P8 G3 G4 L1 R1 O1 C1a C1b G5 G6 P9 P10 L2 R2 O2 C2a C2b
-L3 R3 O3 C3a L4 R4 O4 C3b C4a C4b A0 G9 G7 G8 L5 R5 O5 C5a L6 R6 O6 C5b C6a C6b A1 G10 L9 R9 O9 C9a C9b F0
+SCRIPT = """P0 P1 G0 P3 P4 G1 P2 P5 P6 L0 R0 O0 C0a C0b G2 G3 G4 P7 P8 L1 R1 O1 C1a C1b G5 G6 P9 P10 L2 R2 O2 C2a C2b
+L3 R3 O3 C3a G9 L4 R4 O4 C3b G7 G8 C4a C4b A0 L5 R5 O5 C5a L6 R6 O6 C5b C6a C6b A1 G10 L9 R9 O9 C9a C9b F0
 L7 R7 O7 C7a L8 R8 O8 C7b C8a C8b A2 F1 L10 R10 O10 C10a C10b W F2"""
 
 

time: 190 us -> 191 us (level)
  the two profiles are of different devices: /device:TPU:1 before, /device:TPU:2 now
where the time goes in v10:
time: 191 us
  Pallas kernels  191 us (100%)
    pallas_call x1, Pallas kernels, local_product(): pl.pallas_call(functools.partial(kernel, nz, ny), name='stationary_a', ou...  188 us

profile of v10, /device:TPU:2, one launch (start us, length us, event | category | flops | bytes accessed | tf_op | source)
XLA Modules:
  0.0 190.7 jit_solution(13164808432055640511)
XLA Ops:
  0.0 188.1 %stationary_a.1.src_ref = bf16[256,4096]{1,0:T(8,128)(2,1)} custom-call(bf16[2048,4096]{1,0:T(8,128)(2,1)} %a_ref.1, bf16[2048,4096]{1,0:T(8,128)(2,1)} %b_ref.1), custom_call_target="tpu_custom_call" | custom-call | tf_op jit(solution)/shard_map/stationary_a/pallas_call | solution.py:278
  188.1 2.4 %copy_out.1 = bf16[256,4096]{1,0:T(8,128)(2,1)} custom-call(bf16[256,4096]{1,0:T(8,128)(2,1)} %stationary_a.1.src_ref), custom_call_target="tpu_custom_call" | custom-call | tf_op jit(solution)/shard_map/copy_out/pallas_call | solution.py:260

commit v11 on v10

--- a/solution.py
+++ b/solution.py
@@ -13,8 +13,8 @@
 GROUPS = [(0, 4), (4, 4), (8, 8), (0, 8)]
 NG = 3
 SLOT = {2: 0, 1: 1, 3: 2, 0: 0}
-SCRIPT = """P0 P1 G0 P3 P4 G1 P2 P5 P6 L0 R0 O0 C0a C0b G2 G3 G4 P7 P8 L1 R1 O1 C1a C1b G5 G6 P9 P10 L2 R2 O2 C2a C2b
-L3 R3 O3 C3a G9 L4 R4 O4 C3b G7 G8 C4a C4b A0 L5 R5 O5 C5a L6 R6 O6 C5b C6a C6b A1 G10 L9 R9 O9 C9a C9b F0
+SCRIPT = """P0 P3 P4 P1 P5 P6 G0 P2 G1 L0 R0 O0 C0a G2 C0b P7 P8 G3 G4 L1 R1 O1 C1a C1b G5 G6 P9 P10 L2 R2 O2 C2a C2b
+L3 R3 O3 C3a L4 R4 O4 C3b C4a C4b A0 G7 G8 G9 L5 R5 O5 C5a L6 R6 O6 C5b C6a C6b A1 G10 L9 R9 O9 C9a C9b F0
 L7 R7 O7 C7a L8 R8 O8 C7b C8a C8b A2 F1 L10 R10 O10 C10a C10b W F2"""
 
 

time: 191 us -> 197 us (1.031)
  the two profiles are of different devices: /device:TPU:2 before, /device:TPU:1 now
where the time goes in v11:
time: 197 us; the launch traced here: 196 us
  Pallas kernels  196 us (99%)
    pallas_call x1, Pallas kernels, local_product(): pl.pallas_call(functools.partial(kernel, nz, ny), name='stationary_a', ou...  194 us

profile of v11, /device:TPU:1, one launch (start us, length us, event | category | flops | bytes accessed | tf_op | source)
XLA Modules:
  0.0 196.3 jit_solution(553606935215262858)
XLA Ops:
  0.0 193.7 %stationary_a.1.src_ref = bf16[256,4096]{1,0:T(8,128)(2,1)} custom-call(bf16[2048,4096]{1,0:T(8,128)(2,1)} %a_ref.1, bf16[2048,4096]{1,0:T(8,128)(2,1)} %b_ref.1), custom_call_target="tpu_custom_call" | custom-call | tf_op jit(solution)/shard_map/stationary_a/pallas_call | solution.py:278
  193.7 2.4 %copy_out.1 = bf16[256,4096]{1,0:T(8,128)(2,1)} custom-call(bf16[256,4096]{1,0:T(8,128)(2,1)} %stationary_a.1.src_ref), custom_call_target="tpu_custom_call" | custom-call | tf_op jit(solution)/shard_map/copy_out/pallas_call | solution.py:260

commit v12 on v11

--- a/solution.py
+++ b/solution.py
@@ -14,7 +14,7 @@
 NG = 3
 SLOT = {2: 0, 1: 1, 3: 2, 0: 0}
 SCRIPT = """P0 P3 P4 P1 P5 P6 G0 P2 G1 L0 R0 O0 C0a G2 C0b P7 P8 G3 G4 L1 R1 O1 C1a C1b G5 G6 P9 P10 L2 R2 O2 C2a C2b
-L3 R3 O3 C3a L4 R4 O4 C3b C4a C4b A0 G7 G8 G9 L5 R5 O5 C5a L6 R6 O6 C5b C6a C6b A1 G10 L9 R9 O9 C9a C9b F0
+L3 R3 O3 C3a L4 R4 O4 C3b C4a C4b A0 G9 G7 G8 L5 R5 O5 C5a L6 R6 O6 C5b C6a C6b A1 G10 L9 R9 O9 C9a C9b F0
 L7 R7 O7 C7a L8 R8 O8 C7b C8a C8b A2 F1 L10 R10 O10 C10a C10b W F2"""
 
 

time: 197 us -> 186 us (0.944)
  Pallas kernels: 196 us -> 184 us
    pallas_call x1, Pallas kernels: 194 us -> 182 us  [local_product(): pl.pallas_call(functools.partial(kernel, nz, ny), name='stationary_a', ou...]
where the time goes in v12:
time: 186 us; the launch traced here: 184 us
  Pallas kernels  184 us (99%)
    pallas_call x1, Pallas kernels, local_product(): pl.pallas_call(functools.partial(kernel, nz, ny), name='stationary_a', ou...  182 us

profile of v12, /device:TPU:1, one launch (start us, length us, event | category | flops | bytes accessed | tf_op | source)
XLA Modules:
  0.0 184.5 jit_solution(14307415938277448124)
XLA Ops:
  0.0 181.9 %stationary_a.1.src_ref = bf16[256,4096]{1,0:T(8,128)(2,1)} custom-call(bf16[2048,4096]{1,0:T(8,128)(2,1)} %a_ref.1, bf16[2048,4096]{1,0:T(8,128)(2,1)} %b_ref.1), custom_call_target="tpu_custom_call" | custom-call | tf_op jit(solution)/shard_map/stationary_a/pallas_call | solution.py:278
  181.9 2.4 %copy_out.1 = bf16[256,4096]{1,0:T(8,128)(2,1)} custom-call(bf16[256,4096]{1,0:T(8,128)(2,1)} %stationary_a.1.src_ref), custom_call_target="tpu_custom_call" | custom-call | tf_op jit(solution)/shard_map/copy_out/pallas_call | solution.py:260

commit v13 on v12

--- a/solution.py
+++ b/solution.py
@@ -13,7 +13,7 @@
 GROUPS = [(0, 4), (4, 4), (8, 8), (0, 8)]
 NG = 3
 SLOT = {2: 0, 1: 1, 3: 2, 0: 0}
-SCRIPT = """P0 P3 P4 P1 P5 P6 G0 P2 G1 L0 R0 O0 C0a G2 C0b P7 P8 G3 G4 L1 R1 O1 C1a C1b G5 G6 P9 P10 L2 R2 O2 C2a C2b
+SCRIPT = """P0 P3 P4 P1 G0 P2 G1 P5 P6 L0 R0 O0 C0a G2 C0b P7 P8 G3 G4 L1 R1 O1 C1a C1b G5 G6 P9 P10 L2 R2 O2 C2a C2b
 L3 R3 O3 C3a L4 R4 O4 C3b C4a C4b A0 G9 G7 G8 L5 R5 O5 C5a L6 R6 O6 C5b C6a C6b A1 G10 L9 R9 O9 C9a C9b F0
 L7 R7 O7 C7a L8 R8 O8 C7b C8a C8b A2 F1 L10 R10 O10 C10a C10b W F2"""
 

time: 186 us -> 185 us (level)
  no operation moved by 1% of the time
where the time goes in v13:
time: 185 us
  Pallas kernels  185 us (100%)
    pallas_call x1, Pallas kernels, local_product(): pl.pallas_call(functools.partial(kernel, nz, ny), name='stationary_a', ou...  182 us

profile of v13, /device:TPU:1, one launch (start us, length us, event | category | flops | bytes accessed | tf_op | source)
XLA Modules:
  0.0 184.9 jit_solution(205268849799656303)
XLA Ops:
  0.0 182.3 %stationary_a.1.src_ref = bf16[256,4096]{1,0:T(8,128)(2,1)} custom-call(bf16[2048,4096]{1,0:T(8,128)(2,1)} %a_ref.1, bf16[2048,4096]{1,0:T(8,128)(2,1)} %b_ref.1), custom_call_target="tpu_custom_call" | custom-call | tf_op jit(solution)/shard_map/stationary_a/pallas_call | solution.py:278
  182.3 2.4 %copy_out.1 = bf16[256,4096]{1,0:T(8,128)(2,1)} custom-call(bf16[256,4096]{1,0:T(8,128)(2,1)} %stationary_a.1.src_ref), custom_call_target="tpu_custom_call" | custom-call | tf_op jit(solution)/shard_map/copy_out/pallas_call | solution.py:260

commit v14 on v13

--- a/solution.py
+++ b/solution.py
@@ -123,20 +123,38 @@
 
     def half_matmul(n, h):
         t, group = PIECES[n]
+        k_own = pl.ds(pl.multiple_of(c * half_k, half_k), half_k)
+        k_other = pl.ds(pl.multiple_of((1 - c) * half_k, half_k), half_k)
+        split = t == 2 and h == 0
+
+        def block_rows(d):
+            return pl.ds(pl.multiple_of(d * half + h * mblk, mblk), mblk)
+
+        def product(r, ks):
+            return jnp.dot(abuf[r, ks], bbuf[t, ks, columns(n)], preferred_element_type=jnp.float32)
+
+        if n == 0 and h == 0:
+            pltpu.make_async_copy(abuf, abuf, a_sem).wait()
+        if split:
+            def own_half(d, carry):
+                pbuf[SLOT[t], block_rows(d), columns(n)] = product(block_rows(d), k_own)
+                return carry
+
+            lax.fori_loop(0, 2, own_half, 0)
         if h == 0:
             ref = lane(n, 1 - c)
             remote(ref, ref, b_send, s_recv.at[n], sibling).wait_recv()
-            if n == 0:
-                pltpu.make_async_copy(abuf, abuf, a_sem).wait()
             if t == 0:
                 for m in (0, 1) if group == 3 else (2,):
                     ref = pbuf.at[0, :, group_columns(m)]
                     remote(ref, ref, op_send.at[m], op_recv.at[m, 0], sibling).wait_send()
 
         def body(d, carry):
-            r = pl.ds(pl.multiple_of(d * half + h * mblk, mblk), mblk)
-            pbuf[SLOT[t], r, columns(n)] = jnp.dot(abuf[r, :], bbuf[t, :, columns(n)],
-                                                   preferred_element_type=jnp.float32)
+            r = block_rows(d)
+            if split:
+                pbuf[SLOT[t], r, columns(n)] = pbuf[SLOT[t], r, columns(n)] + product(r, k_other)
+            else:
+                pbuf[SLOT[t], r, columns(n)] = product(r, pl.ds(0, 2 * half_k))
             if t == 2:
                 opposite_copy(group, d, h).start()
             return carry

time: 185 us -> 187 us (1.011)
  no operation moved by 1% of the time
where the time goes in v14:
time: 187 us
  Pallas kernels  186 us (99%)
    pallas_call x1, Pallas kernels, local_product(): pl.pallas_call(functools.partial(kernel, nz, ny), name='stationary_a', ou...  184 us

profile of v14, /device:TPU:1, one launch (start us, length us, event | category | flops | bytes accessed | tf_op | source)
XLA Modules:
  0.0 186.7 jit_solution(3568502995735558334)
XLA Ops:
  0.0 184.1 %stationary_a.1.src_ref = bf16[256,4096]{1,0:T(8,128)(2,1)} custom-call(bf16[2048,4096]{1,0:T(8,128)(2,1)} %a_ref.1, bf16[2048,4096]{1,0:T(8,128)(2,1)} %b_ref.1), custom_call_target="tpu_custom_call" | custom-call | tf_op jit(solution)/shard_map/stationary_a/pallas_call | solution.py:296
  184.1 2.4 %copy_out.1 = bf16[256,4096]{1,0:T(8,128)(2,1)} custom-call(bf16[256,4096]{1,0:T(8,128)(2,1)} %stationary_a.1.src_ref), custom_call_target="tpu_custom_call" | custom-call | tf_op jit(solution)/shard_map/copy_out/pallas_call | solution.py:278

commit v15 on v13

--- a/solution.py
+++ b/solution.py
@@ -13,7 +13,7 @@
 GROUPS = [(0, 4), (4, 4), (8, 8), (0, 8)]
 NG = 3
 SLOT = {2: 0, 1: 1, 3: 2, 0: 0}
-SCRIPT = """P0 P3 P4 P1 G0 P2 G1 P5 P6 L0 R0 O0 C0a G2 C0b P7 P8 G3 G4 L1 R1 O1 C1a C1b G5 G6 P9 P10 L2 R2 O2 C2a C2b
+SCRIPT = """P0 P1 G0 P2 P3 P4 G1 P5 P6 L0 R0 O0 C0a G2 C0b P7 P8 G3 G4 L1 R1 O1 C1a C1b G5 G6 P9 P10 L2 R2 O2 C2a C2b
 L3 R3 O3 C3a L4 R4 O4 C3b C4a C4b A0 G9 G7 G8 L5 R5 O5 C5a L6 R6 O6 C5b C6a C6b A1 G10 L9 R9 O9 C9a C9b F0
 L7 R7 O7 C7a L8 R8 O8 C7b C8a C8b A2 F1 L10 R10 O10 C10a C10b W F2"""
 

time: 185 us -> 185 us (level)
  no operation moved by 1% of the time
where the time goes in v15:
time: 185 us
  Pallas kernels  184 us (99%)
    pallas_call x1, Pallas kernels, local_product(): pl.pallas_call(functools.partial(kernel, nz, ny), name='stationary_a', ou...  182 us

profile of v15, /device:TPU:1, one launch (start us, length us, event | category | flops | bytes accessed | tf_op | source)
XLA Modules:
  0.0 184.5 jit_solution(10328189659245664653)
XLA Ops:
  0.0 181.9 %stationary_a.1.src_ref = bf16[256,4096]{1,0:T(8,128)(2,1)} custom-call(bf16[2048,4096]{1,0:T(8,128)(2,1)} %a_ref.1, bf16[2048,4096]{1,0:T(8,128)(2,1)} %b_ref.1), custom_call_target="tpu_custom_call" | custom-call | tf_op jit(solution)/shard_map/stationary_a/pallas_call | solution.py:278
  181.9 2.4 %copy_out.1 = bf16[256,4096]{1,0:T(8,128)(2,1)} custom-call(bf16[256,4096]{1,0:T(8,128)(2,1)} %stationary_a.1.src_ref), custom_call_target="tpu_custom_call" | custom-call | tf_op jit(solution)/shard_map/copy_out/pallas_call | solution.py:260

commit v16 on v15

--- a/solution.py
+++ b/solution.py
@@ -13,7 +13,7 @@
 GROUPS = [(0, 4), (4, 4), (8, 8), (0, 8)]
 NG = 3
 SLOT = {2: 0, 1: 1, 3: 2, 0: 0}
-SCRIPT = """P0 P1 G0 P2 P3 P4 G1 P5 P6 L0 R0 O0 C0a G2 C0b P7 P8 G3 G4 L1 R1 O1 C1a C1b G5 G6 P9 P10 L2 R2 O2 C2a C2b
+SCRIPT = """P0 P1 G0 P2 P3 P4 G1 P5 P6 L0 R0 O0 C0a C0b G2 P7 P8 G3 G4 L1 R1 O1 C1a C1b G5 G6 P9 P10 L2 R2 O2 C2a C2b
 L3 R3 O3 C3a L4 R4 O4 C3b C4a C4b A0 G9 G7 G8 L5 R5 O5 C5a L6 R6 O6 C5b C6a C6b A1 G10 L9 R9 O9 C9a C9b F0
 L7 R7 O7 C7a L8 R8 O8 C7b C8a C8b A2 F1 L10 R10 O10 C10a C10b W F2"""
 

time: 185 us -> 189 us (1.022)
  Pallas kernels: 184 us -> 189 us
    pallas_call x1, Pallas kernels: 182 us -> 186 us  [local_product(): pl.pallas_call(functools.partial(kernel, nz, ny), name='stationary_a', ou...]
where the time goes in v16:
time: 189 us
  Pallas kernels  189 us (100%)
    pallas_call x1, Pallas kernels, local_product(): pl.pallas_call(functools.partial(kernel, nz, ny), name='stationary_a', ou...  186 us

profile of v16, /device:TPU:1, one launch (start us, length us, event | category | flops | bytes accessed | tf_op | source)
XLA Modules:
  0.0 189.1 jit_solution(5004283516528163124)
XLA Ops:
  0.0 186.5 %stationary_a.1.src_ref = bf16[256,4096]{1,0:T(8,128)(2,1)} custom-call(bf16[2048,4096]{1,0:T(8,128)(2,1)} %a_ref.1, bf16[2048,4096]{1,0:T(8,128)(2,1)} %b_ref.1), custom_call_target="tpu_custom_call" | custom-call | tf_op jit(solution)/shard_map/stationary_a/pallas_call | solution.py:278
  186.5 2.4 %copy_out.1 = bf16[256,4096]{1,0:T(8,128)(2,1)} custom-call(bf16[256,4096]{1,0:T(8,128)(2,1)} %stationary_a.1.src_ref), custom_call_target="tpu_custom_call" | custom-call | tf_op jit(solution)/shard_map/copy_out/pallas_call | solution.py:260

commit v17 on v16

--- a/solution.py
+++ b/solution.py
@@ -13,7 +13,7 @@
 GROUPS = [(0, 4), (4, 4), (8, 8), (0, 8)]
 NG = 3
 SLOT = {2: 0, 1: 1, 3: 2, 0: 0}
-SCRIPT = """P0 P1 G0 P2 P3 P4 G1 P5 P6 L0 R0 O0 C0a C0b G2 P7 P8 G3 G4 L1 R1 O1 C1a C1b G5 G6 P9 P10 L2 R2 O2 C2a C2b
+SCRIPT = """P0 P1 G0 P2 P3 P4 G1 P5 P6 L0 R0 O0 C0a G2 C0b L1 R1 O1 P7 P8 G3 G4 C1a C1b G5 G6 P9 P10 L2 R2 O2 C2a C2b
 L3 R3 O3 C3a L4 R4 O4 C3b C4a C4b A0 G9 G7 G8 L5 R5 O5 C5a L6 R6 O6 C5b C6a C6b A1 G10 L9 R9 O9 C9a C9b F0
 L7 R7 O7 C7a L8 R8 O8 C7b C8a C8b A2 F1 L10 R10 O10 C10a C10b W F2"""
 

time: 189 us -> 186 us (0.984)
  Pallas kernels: 189 us -> 185 us
    pallas_call x1, Pallas kernels: 186 us -> 183 us  [local_product(): pl.pallas_call(functools.partial(kernel, nz, ny), name='stationary_a', ou...]
where the time goes in v17:
time: 186 us; the launch traced here: 185 us
  Pallas kernels  185 us (99%)
    pallas_call x1, Pallas kernels, local_product(): pl.pallas_call(functools.partial(kernel, nz, ny), name='stationary_a', ou...  183 us

profile of v17, /device:TPU:1, one launch (start us, length us, event | category | flops | bytes accessed | tf_op | source)
XLA Modules:
  0.0 185.2 jit_solution(17266744837964392511)
XLA Ops:
  0.0 182.6 %stationary_a.1.src_ref = bf16[256,4096]{1,0:T(8,128)(2,1)} custom-call(bf16[2048,4096]{1,0:T(8,128)(2,1)} %a_ref.1, bf16[2048,4096]{1,0:T(8,128)(2,1)} %b_ref.1), custom_call_target="tpu_custom_call" | custom-call | tf_op jit(solution)/shard_map/stationary_a/pallas_call | solution.py:278
  182.6 2.4 %copy_out.1 = bf16[256,4096]{1,0:T(8,128)(2,1)} custom-call(bf16[256,4096]{1,0:T(8,128)(2,1)} %stationary_a.1.src_ref), custom_call_target="tpu_custom_call" | custom-call | tf_op jit(solution)/shard_map/copy_out/pallas_call | solution.py:260

commit v18 on v17

--- a/solution.py
+++ b/solution.py
@@ -13,7 +13,7 @@
 GROUPS = [(0, 4), (4, 4), (8, 8), (0, 8)]
 NG = 3
 SLOT = {2: 0, 1: 1, 3: 2, 0: 0}
-SCRIPT = """P0 P1 G0 P2 P3 P4 G1 P5 P6 L0 R0 O0 C0a G2 C0b L1 R1 O1 P7 P8 G3 G4 C1a C1b G5 G6 P9 P10 L2 R2 O2 C2a C2b
+SCRIPT = """P0 P1 G0 P2 P3 P4 G1 P5 P6 L0 R0 O0 C0a G2 C0b G3 G4 P7 P8 L1 R1 O1 C1a C1b G5 G6 P9 P10 L2 R2 O2 C2a C2b
 L3 R3 O3 C3a L4 R4 O4 C3b C4a C4b A0 G9 G7 G8 L5 R5 O5 C5a L6 R6 O6 C5b C6a C6b A1 G10 L9 R9 O9 C9a C9b F0
 L7 R7 O7 C7a L8 R8 O8 C7b C8a C8b A2 F1 L10 R10 O10 C10a C10b W F2"""
 

time: 186 us -> 186 us (level)
  no operation moved by 1% of the time
where the time goes in v18:
time: 186 us; the launch traced here: 185 us
  Pallas kernels  185 us (99%)
    pallas_call x1, Pallas kernels, local_product(): pl.pallas_call(functools.partial(kernel, nz, ny), name='stationary_a', ou...  182 us

profile of v18, /device:TPU:1, one launch (start us, length us, event | category | flops | bytes accessed | tf_op | source)
XLA Modules:
  0.0 185.0 jit_solution(12891602058473476049)
XLA Ops:
  0.0 182.4 %stationary_a.1.src_ref = bf16[256,4096]{1,0:T(8,128)(2,1)} custom-call(bf16[2048,4096]{1,0:T(8,128)(2,1)} %a_ref.1, bf16[2048,4096]{1,0:T(8,128)(2,1)} %b_ref.1), custom_call_target="tpu_custom_call" | custom-call | tf_op jit(solution)/shard_map/stationary_a/pallas_call | solution.py:278
  182.4 2.4 %copy_out.1 = bf16[256,4096]{1,0:T(8,128)(2,1)} custom-call(bf16[256,4096]{1,0:T(8,128)(2,1)} %stationary_a.1.src_ref), custom_call_target="tpu_custom_call" | custom-call | tf_op jit(solution)/shard_map/copy_out/pallas_call | solution.py:260
